TPU v7x, 512 devices: a 8x2x16 block of a 8x8x16 slice. The times are simulated.
512 devices in a mesh: groups: 2 (over y), wide: 128 (over x, z), narrow: 2 (over core).
Axes of the slice: x: 8, y: 2, z: 16, core: 2. Of those that a mesh axis runs over, the one named last changes fastest.
The devices are a block of a 8x8x16 slice.
Arguments:
- hidden_in: bfloat16 [102400, 1024], P(('groups', 'wide')), parts along dimension 0, may hold values from -6 to 6
- ffn_gain: bfloat16 [1024], replicated, may hold values from 0.5 to 1.5
- wi_gate: bfloat16 [1024, 2816], P('wide', 'narrow'), may hold values from -0.1875 to 0.1875
- wi_up: bfloat16 [1024, 2816], P('wide', 'narrow'), may hold values from -0.1875 to 0.1875
- wo_down: bfloat16 [2816, 1024], P('narrow', 'wide'), may hold values from -0.109375 to 0.109375
- final_gain: bfloat16 [1024], replicated, may hold values from 0.5 to 1.5
- key_w: bfloat16 [1024, 1024], P('wide', 'narrow'), may hold values from -0.1875 to 0.1875
- value_w: bfloat16 [1024, 1024], P('wide', 'narrow'), may hold values from -0.1875 to 0.1875
- query_w: bfloat16 [1024, 1024], P('wide', 'narrow'), may hold values from -8 to 8
- out_w: bfloat16 [1024, 1024], P('narrow', 'wide'), may hold values from -0.1875 to 0.1875
- dec_gain: bfloat16 [1024], replicated, may hold values from 0.5 to 1.5
- embed: bfloat16 [32128, 1024], P('wide'), may hold values from -6 to 6
- lengths: int32 [512], P(('groups', 'wide')), parts along dimension 0, may hold values from 40 to 200
- answer_ids: int32 [8, 32], P('groups'), parts along dimension 0, may hold values from 0 to 32127
Outputs:
- memory: bfloat16 [102400, 1024], P(('groups', 'wide')), parts along dimension 0
- decoded: bfloat16 [256, 1024], P('groups', 'narrow'), parts along dimension 0
There are 2 independent parts, one for each index of `groups`. A program takes and returns all parts, laid end to end along the dimension named above; an argument that names none is the same for every part. Nothing has to cross between parts.
All inputs are finite; a program needn't handle non-finite values.
Results may differ from a plain program's by a relative error of at most 0.0095.
The roundings to bfloat16 on the way count: a program that leaves them out, or rounds other values in their place, can miss the bound.
Values may be sent and summed in bfloat16 or wider, within the bound.
A program may use at most 64 MiB of HBM per device.

v0:
```python
import math

import jax
import jax.numpy as jnp
from jax import lax
from jax.sharding import Mesh
from jax.sharding import PartitionSpec as P

HEAD_DIM = 64
QUEST = 4
WIDE = ("wide_0", "wide_1")
GROUPS_WIDE = ("groups", "wide_0", "wide_1")


EPS = 1e-06
FLOOR = -1e30


def in_one_piece(arrays, axis, dim, along):
    ends, at = ([], 0)
    for a in arrays[:-1]:
        at += a.shape[along]
        ends.append(at)
    both = jnp.concatenate(arrays, axis=along)
    return tuple(jnp.split(lax.all_gather(both, axis, axis=dim, tiled=True), ends, axis=along))


def in_order(tiles, dim):
    tiles = jnp.moveaxis(tiles, 0, dim)
    lengths = tiles.shape
    return tiles.reshape(*lengths[:dim], lengths[dim] * lengths[dim + 1], *lengths[dim + 2 :])


def all_blocks(x, axes, turns):
    tiles = x
    for k in turns:
        tiles = lax.all_gather(tiles, axes[k])
    done = turns[::-1]
    back = [done.index(k) for k in range(len(axes))]
    tiles = tiles.transpose(*back, *range(len(axes), tiles.ndim))
    return tiles.reshape(-1, *x.shape)


def whole_of(x, axes, turns, dim):
    return in_order(all_blocks(x, axes, turns), dim)


def from_everyone(x, axis):
    copies = jnp.broadcast_to(x, (lax.axis_size(axis), *x.shape))
    return lax.all_to_all(copies, axis, split_axis=0, concat_axis=0, tiled=True)


def over_copies(x, axis):
    return from_everyone(x, axis).sum(axis=0)


def collected_together(x, axis):
    leaves = jax.tree.leaves(x)
    turns = sorted(range(len(leaves)), key=lambda k: -leaves[k].size)
    width = (1, *leaves[turns[0]].shape)[-1]
    lines = [
        jnp.pad(leaves[k].reshape(-1), (0, -leaves[k].size % width)).reshape(-1, width)
        for k in turns
    ]
    both, at, found = (lax.all_gather(jnp.concatenate(lines), axis), 0, {})
    for k, line in zip(turns, lines):
        piece = both[:, at : at + len(line)].reshape(len(both), -1)
        found[k] = piece[:, : leaves[k].size].reshape(-1, *leaves[k].shape)
        at += len(line)
    numbers = iter(range(len(leaves)))
    return jax.tree.map(lambda _: found[next(numbers)], x)


def joined_all(x, axes, combine):
    for axis in axes:
        pieces = collected_together(x, axis)
        x = jax.tree.map(lambda part: part[0], pieces)
        for k in range(1, lax.axis_size(axis)):
            x = combine(x, jax.tree.map(lambda part: part[k], pieces))
    return x


def split_up(x, dim, devices):
    lengths = x.shape
    tiles = x.reshape(*lengths[:dim], devices, lengths[dim] // devices, *lengths[dim + 1 :])
    return jnp.moveaxis(tiles, dim, 0)


def sum_at_owner(x, axis, dim):
    tiles = split_up(x, dim, lax.axis_size(axis))
    arrived = lax.all_to_all(tiles, axis, split_axis=0, concat_axis=0, tiled=True)
    return arrived.astype(jnp.float32).sum(axis=0)


def rms_scale(values, gain):
    mean_square = jnp.mean(values * values, axis=-1, keepdims=True)
    return values * lax.rsqrt(mean_square + EPS) * gain.astype(jnp.float32)


def join_partial(first, second):
    top_first, total_first, acc_first = first
    top_second, total_second, acc_second = second
    top = jnp.maximum(top_first, top_second)
    factor_first = jnp.exp(top_first - top)
    factor_second = jnp.exp(top_second - top)
    width = acc_first.shape[1] // top.shape[1]
    total = total_first * factor_first + total_second * factor_second
    acc = acc_first * jnp.repeat(factor_first, width, axis=1) + acc_second * jnp.repeat(
        factor_second, width, axis=1
    )
    return (top, total, acc)


def per_device(
    hidden_in,
    ffn_gain,
    wi_gate,
    wi_up,
    wo_down,
    final_gain,
    key_w,
    value_w,
    query_w,
    out_w,
    dec_gain,
    embed,
    lengths,
    answer_ids,
):
    rows = hidden_in.shape[0]
    resid_in = hidden_in.astype(jnp.float32)
    enc_in = rms_scale(resid_in, ffn_gain).astype(jnp.bfloat16)
    gate_full, up_full = in_one_piece((wi_gate, wi_up), WIDE, 0, 1)
    gate = jnp.dot(enc_in, gate_full, preferred_element_type=jnp.float32)
    up = jnp.dot(enc_in, up_full, preferred_element_type=jnp.float32)
    inner = (jax.nn.gelu(gate, approximate=True) * up).astype(jnp.bfloat16)
    down_full = whole_of(wo_down, WIDE, (0, 1), 1)
    partial_down = jnp.dot(inner, down_full, preferred_element_type=jnp.float32)
    resid = resid_in + over_copies(partial_down, "narrow")
    memory = rms_scale(resid, final_gain).astype(jnp.bfloat16)
    pass_dev = lengths.shape[0]
    per_question = pass_dev * lax.axis_size(WIDE) // QUEST
    question = lax.axis_index(WIDE) * pass_dev // per_question
    answers = answer_ids.shape[1]
    qrows = answer_ids.shape[0] * answers
    vocab_rows = embed.shape[0]
    local_ids = answer_ids.reshape(qrows) - lax.axis_index(WIDE) * vocab_rows
    onehot = (local_ids[:, None] == jnp.arange(vocab_rows, dtype=jnp.int32)[None, :]).astype(
        jnp.bfloat16
    )
    embedded = lax.psum(jnp.dot(onehot, embed, preferred_element_type=jnp.float32), WIDE)
    dec_in = rms_scale(embedded, dec_gain).astype(jnp.bfloat16)
    own_rows = lax.dynamic_slice_in_dim(dec_in, question * answers, answers, 0)
    proj_cols = key_w.shape[1]
    key_full, value_full, query_full = in_one_piece((key_w, value_w, query_w), WIDE, 0, 1)
    keys_sum = jnp.dot(memory, key_full, preferred_element_type=jnp.float32)
    values_sum = jnp.dot(memory, value_full, preferred_element_type=jnp.float32)
    query_sum = jnp.dot(own_rows, query_full, preferred_element_type=jnp.float32)
    keys = keys_sum.astype(jnp.bfloat16)
    values = values_sum.astype(jnp.bfloat16)
    query = query_sum.astype(jnp.bfloat16)
    heads_local = proj_cols // HEAD_DIM
    query_three = query.reshape(answers, heads_local, HEAD_DIM)
    keys_three = keys.reshape(rows, heads_local, HEAD_DIM)
    values_three = values.reshape(rows, heads_local, HEAD_DIM).astype(jnp.float32)
    scores = jnp.einsum(
        "ahd,khd->ahk", query_three, keys_three, preferred_element_type=jnp.float32
    ) * (1.0 / math.sqrt(HEAD_DIM))
    passage_len = rows // pass_dev
    live = (jnp.arange(passage_len, dtype=jnp.int32)[None, :] < lengths[:, None]).reshape(rows)
    scores = jnp.where(live[None, None, :], scores, FLOOR)
    top = jnp.max(scores, axis=2)
    weights = jnp.exp(scores - top[:, :, None])
    total = jnp.sum(weights, axis=2)
    acc = jnp.einsum("ahk,khd->ahd", weights, values_three).reshape(answers, proj_cols)
    start_row = question * answers
    top_all = lax.dynamic_update_slice_in_dim(
        jnp.full((qrows, heads_local), FLOOR, jnp.float32), top, start_row, 0
    )
    total_all = lax.dynamic_update_slice_in_dim(
        jnp.zeros((qrows, heads_local), jnp.float32), total, start_row, 0
    )
    acc_all = lax.dynamic_update_slice_in_dim(
        jnp.zeros((qrows, proj_cols), jnp.float32), acc, start_row, 0
    )
    top_all, total_all, acc_all = joined_all((top_all, total_all, acc_all), WIDE, join_partial)
    attended = (acc_all / jnp.repeat(total_all, HEAD_DIM, axis=1)).astype(jnp.bfloat16)
    out_full = whole_of(out_w, WIDE, (0, 1), 1)
    partial_out = jnp.dot(attended, out_full, preferred_element_type=jnp.float32)
    share_out = sum_at_owner(partial_out.astype(jnp.bfloat16), "narrow", 1)
    out_half = share_out.shape[1]
    embedded_half = lax.dynamic_slice_in_dim(
        embedded, lax.axis_index("narrow") * out_half, out_half, 1
    )
    decoded = (embedded_half + share_out).astype(jnp.bfloat16)
    return (memory, decoded)


def solution(mesh):
    torus = Mesh(
        mesh.devices.reshape(mesh.shape["groups"], 8, 16, mesh.shape["narrow"]),
        ("groups", "wide_0", "wide_1", "narrow"),
    )
    return jax.shard_map(
        per_device,
        mesh=torus,
        in_specs=(
            P(GROUPS_WIDE, None),
            P(),
            P(WIDE, "narrow"),
            P(WIDE, "narrow"),
            P("narrow", WIDE),
            P(),
            P(WIDE, "narrow"),
            P(WIDE, "narrow"),
            P(WIDE, "narrow"),
            P("narrow", WIDE),
            P(),
            P(WIDE, None),
            P(GROUPS_WIDE),
            P("groups", None),
        ),
        out_specs=(P(GROUPS_WIDE, None), P("groups", "narrow")),
        check_vma=False,
    )
```

profile of v0, /device:TPU:65, one launch (start us, length us, event | category | flops | bytes accessed | tf_op | source)
XLA Modules:
  0.0 730.1 jit_solution(12528337579370721748)
XLA Ops:
  10.3 23.2 %all-gather = bf16[11264,8]{0,1:T(8,128)(2,1)} all-gather(bf16[1408,8]{0,1:T(8,128)(2,1)} %param.18), channel_id=2, replica_groups=mesh['groups'=2,'wide_0'=8,'wide_1'=16,'narrow'=2] {'wide_0'}, dimensions={0}, use_global_device_ids=true | all-gather | bytes 202752 | tf_op jit(solution)/shard_map/all_gather | solution.py:37
  38.4 277.3 %all-reduce.2.cloned.1.call-done = f32[128,1024]{1,0:T(8,128)} async-done(((f32[128,1024]{1,0:T(8,128)}), f32[128,1024]{1,0:T(8,128)}) %all-reduce.2.cloned.1.call-update) | async-done | bytes 524304 | tf_op jit(solution)/shard_map/psum | solution.py:151
  317.0 3.8 copy.413
  320.8 1.5 convolution_convert_fusion.3
  323.1 111.4 %all-gather.15.cloned.1.call-done = bf16[1024,2816]{1,0:T(8,128)(2,1)} async-done(((bf16[8,2816]{1,0:T(8,128)(2,1)}), bf16[1024,2816]{1,0:T(8,128)(2,1)}) %all-gather.15.cloned.1.call-update) | async-done | bytes 5767184 | tf_op jit(solution)/shard_map/all_gather | solution.py:25
  434.4 4.9 fusion.12
  439.4 6.1 fusion.24
  445.9 15.5 %all_to_all.10 = f32[2,400,1024]{2,1,0:T(8,128)} all-to-all(f32[2,400,1024]{2,1,0:T(8,128)S(1)} %broadcast_in_dim.170), channel_id=1, replica_groups=mesh['groups'=2,'wide_0'=8,'wide_1'=16,'narrow'=2] {'narrow'}, dimensions={0} | all-to-all | bytes 6553600 | tf_op jit(solution)/shard_map/all_to_all | solution.py:50
  461.4 2.4 reduce_sum.55
  465.3 1.8 convolution_convert_fusion
  468.3 1.8 convolution_convert_fusion.1
  471.7 21.1 %all-gather.4 = bf16[4096,8]{0,1:T(8,128)(2,1)} all-gather(bf16[512,8]{0,1:T(8,128)(2,1)S(1)} %copy-done.8), channel_id=6, replica_groups=mesh['groups'=2,'wide_0'=8,'wide_1'=16,'narrow'=2] {'wide_0'}, dimensions={0}, use_global_device_ids=true | all-gather | bytes 73728 | tf_op jit(solution)/shard_map/all_gather | solution.py:37
  493.2 16.7 %all-gather.23.cloned.1.call-done = f32[8,132,512]{2,1,0:T(8,128)} async-done(((f32[1,132,512]{2,1,0:T(8,128)}), f32[8,132,512]{2,1,0:T(8,128)}) %all-gather.23.cloned.1.call-update) | async-done | bytes 2162704 | tf_op jit(solution)/shard_map/all_gather | solution.py:65
  511.2 2.6 fusion.96
  515.5 1.8 copy.514
  522.7 54.6 %all-gather.21.cloned.1.call-done = bf16[128,512,8]{1,2,0:T(8,128)(2,1)} async-done(((bf16[8,512,8]{1,2,0:T(8,128)(2,1)}), bf16[128,512,8]{1,2,0:T(8,128)(2,1)}) %all-gather.21.cloned.1.call-update) | async-done | bytes 1048592 | tf_op jit(solution)/shard_map/all_gather | solution.py:37
  578.6 79.3 %all-gather.25.cloned.1.call-done = f32[16,132,512]{2,1,0:T(8,128)} async-done(((f32[1,132,512]{2,1,0:T(8,128)}), f32[16,132,512]{2,1,0:T(8,128)}) %all-gather.25.cloned.1.call-update) | async-done | bytes 4325392 | tf_op jit(solution)/shard_map/all_gather | solution.py:65
  657.8 3.8 fusion.94
  663.3 1.8 copy.531
  665.1 1.8 copy.530
  666.9 1.8 copy.529
  668.7 1.8 copy.528
  670.5 1.8 copy.527
  672.3 1.8 copy.526
  674.1 1.8 copy.525
  675.8 1.8 copy.524
  677.6 1.8 copy.523
  679.4 1.8 copy.522
  681.2 1.8 copy.521
  685.5 1.6 fusion.92
  706.2 2.6 divide_convert_fusion
  709.3 12.7 %all_to_all.11 = bf16[2,128,512]{2,1,0:T(8,128)(2,1)S(1)} all-to-all(bf16[2,128,512]{2,1,0:T(8,128)(2,1)S(1)} %bitcast.360), channel_id=1, replica_groups=mesh['groups'=2,'wide_0'=8,'wide_1'=16,'narrow'=2] {'narrow'}, dimensions={0} | all-to-all | bytes 524288 | tf_op jit(solution)/shard_map/all_to_all | solution.py:91
  (186 shorter events, 47.7 us)
Async XLA Ops:
  8.0 1.0 copy-start
  8.1 30.0 %copy-start.9 = (bf16[1024]{0:T(1024)(128)(2,1)S(1)}, bf16[1024]{0:T(1024)(128)(2,1)}, u32[]{:S(2)}) copy-start(bf16[1024]{0:T(1024)(128)(2,1)} %param.24) | copy-start | bytes 6148
  8.1 30.0 %copy-start.10 = (s32[2]{0:T(128)S(1)}, s32[2]{0:T(128)}, u32[]{:S(2)}) copy-start(s32[2]{0:T(128)} %param.26) | copy-start | bytes 28
  8.1 30.1 %copy-start.1 = (bf16[400,1024]{1,0:T(8,128)(2,1)S(1)}, bf16[400,1024]{1,0:T(8,128)(2,1)}, u32[]{:S(2)}) copy-start(bf16[400,1024]{1,0:T(8,128)(2,1)} %param.14) | copy-start | bytes 2457604
  8.1 307.7 %all-reduce.2.cloned.1.call-start = ((), (), s32[]{:S(2)}) async-start(), calls=%async_computation.3 | async-start | bytes 1048576 | tf_op jit(solution)/shard_map/psum | solution.py:151
  10.2 306.8 %all-gather.19.cloned.1.call-start = ((), (), s32[]{:S(2)}) async-start(), calls=%async_computation.5 | async-start | bytes 3063808 | tf_op jit(solution)/shard_map/all_gather | solution.py:37
  33.6 287.2 %all-gather.17.cloned.1.call-start = ((), (), s32[]{:S(2)}) async-start(), calls=%async_computation.4 | async-start | bytes 3170304 | tf_op jit(solution)/shard_map/all_gather | solution.py:25
  35.0 399.4 %all-gather.15.cloned.1.call-start = ((), (), s32[]{:S(2)}) async-start(), calls=%async_computation.2 | async-start | bytes 5812224 | tf_op jit(solution)/shard_map/all_gather | solution.py:25
  36.6 473.3 %all-gather.23.cloned.1.call-start = ((), (), s32[]{:S(2)}) async-start(), calls=%async_computation.7 | async-start | bytes 2506752 | tf_op jit(solution)/shard_map/all_gather | solution.py:65
  317.0 3.8 copy-start.2
  464.4 0.9 copy-start.3
  465.2 2.1 copy-start.5
  467.1 1.1 copy-start.4
  470.1 1.6 copy-start.8
  471.6 105.6 %all-gather.21.cloned.1.call-start = ((), (), s32[]{:S(2)}) async-start(), calls=%async_computation.6 | async-start | bytes 1114112 | tf_op jit(solution)/shard_map/all_gather | solution.py:37
  492.9 164.9 %all-gather.25.cloned.1.call-start = ((), (), s32[]{:S(2)}) async-start(), calls=%async_computation.8 | async-start | bytes 4734976 | tf_op jit(solution)/shard_map/all_gather | solution.py:65
  691.4 10.7 %copy-start.6 = (f32[1,2,512]{2,1,0:T(2,128)S(1)}, f32[1,2,512]{2,1,0:T(2,128)}, u32[]{:S(2)}) copy-start(f32[1,2,512]{2,1,0:T(2,128)} %get-tuple-element.67) | copy-start | bytes 12292
  692.2 9.8 %copy-start.7 = (f32[1,2,512]{2,1,0:T(2,128)S(1)}, f32[1,2,512]{2,1,0:T(2,128)}, u32[]{:S(2)}) copy-start(f32[1,2,512]{2,1,0:T(2,128)} %get-tuple-element.76) | copy-start | bytes 12292
Sparse Core Ops, SparseCore 0:
  13.0 302.6 all-reduce.1
  471.8 38.0 all-gather.22
  511.9 65.2 all-gather.20
  579.2 78.5 all-gather.24
Sparse Core Ops, SparseCore 1:
  33.7 106.3 all-gather.18
  143.5 142.1 all-gather.16
  288.5 145.9 all-gather.14
where the time goes:
time: 732 us; the launch traced here: 730 us
  waiting for transfers between devices  540 us (74%)
  blocking collectives  72.5 us (10%)
  local copies, waits for them, and re-layouts  65.7 us (9%)
  matrix products  18.4 us (3%)
  other arithmetic  17 us (2%)
  between operations  16.3 us (2%)
    psum x1, waiting for transfers between devices, per_device(): lax.psum(jnp.dot(onehot, embed, preferred_element_type=jnp.float32), WIDE)  277 us
    all_gather x2, waiting for transfers between devices, in_one_piece(): lax.all_gather(both, axis, axis=dim, tiled=True)  111 us
    all_gather x2, waiting for transfers between devices, collected_together(): both, at, found = (lax.all_gather(jnp.concatenate(lines), axis), 0, {})  95.9 us
    all_gather x2, waiting for transfers between devices, all_blocks(): tiles = lax.all_gather(tiles, axes[k])  54.6 us
    all_gather x2, blocking collectives, all_blocks(): tiles = lax.all_gather(tiles, axes[k])  44.4 us
    unnamed x47, local copies, waits for them, and re-layouts  27.5 us
    squeeze x74, local copies, waits for them, and re-layouts, joined_all(): x = combine(x, jax.tree.map(lambda part: part[k], pieces))  18.4 us
    all_to_all x1, blocking collectives, from_everyone(): return lax.all_to_all(copies, axis, split_axis=0, concat_axis=0, tiled=True)  15.5 us
  transfers between devices with their start and end apart: 7, of which 5 were waited for; matrix products, arithmetic and copies ran while one was open for 4% of the time, Pallas kernels for 0%

commit v1 on v0

v1 whole, which is shorter than its diff:
```python
import functools
import math

import jax
import jax.numpy as jnp
from jax import lax
from jax.experimental import pallas as pl
from jax.experimental.pallas import tpu as pltpu
from jax.sharding import Mesh
from jax.sharding import PartitionSpec as P

HEAD_DIM = 64
QUEST = 4
WIDE = ("wide_0", "wide_1")
GROUPS_WIDE = ("groups", "wide_0", "wide_1")
X, Z, CORE = "wide_0", "wide_1", "narrow"
NX, NZ = 8, 16
MESH = pl.DeviceIdType.MESH

EPS = 1e-06
FLOOR = -1e30


def rms_scale(values, gain):
    mean_square = jnp.mean(values * values, axis=-1, keepdims=True)
    return values * lax.rsqrt(mean_square + EPS) * gain.astype(jnp.float32)


def turn(i, by, n):
    return lax.rem(i + (by + 2 * n), n)


def greet(peers):
    barrier = pltpu.get_barrier_semaphore()
    for peer in peers:
        pl.semaphore_signal(barrier, inc=1, device_id=peer, device_id_type=MESH)
    pl.semaphore_wait(barrier, len(peers))


def others(axis, n, steps=None):
    me = lax.axis_index(axis)
    return [{axis: turn(me, d, n)} for d in (steps or range(1, n))]


def remote(src, dst, send, recv, peer):
    return pltpu.make_async_remote_copy(
        src_ref=src, dst_ref=dst, send_sem=send, recv_sem=recv, device_id=peer, device_id_type=MESH
    )


def gather_kernel(a_ref, b_ref, fa, fb, a1, a2, b1, b2, sends, local):
    x, z = lax.axis_index(X), lax.axis_index(Z)
    greet(others(X, NX, (1, -1)) + others(Z, NZ, (1, -1)))
    own = [
        pltpu.make_async_copy(a_ref, fa.at[x * NZ + z], local.at[0]),
        pltpu.make_async_copy(b_ref, fb.at[x * NZ + z], local.at[1]),
    ]
    for copy in own:
        copy.start()

    def block_a(first, second):
        return turn(x, second, NX) * NZ + turn(z, first, NZ)

    def block_b(first, second):
        return turn(x, first, NX) * NZ + turn(z, second, NZ)

    plans = []
    for index, (src, full, block, axis1, n1, axis2, n2, sem1, sem2) in enumerate(
        ((a_ref, fa, block_a, Z, NZ, X, NX, a1, a2), (b_ref, fb, block_b, X, NX, Z, NZ, b1, b2))
    ):
        width = src.shape[1]
        half = width // 256 * 128
        cuts = (pl.ds(0, half), pl.ds(half, width - half))
        me1, me2 = lax.axis_index(axis1), lax.axis_index(axis2)
        peers1 = tuple({axis1: turn(me1, d, n1)} for d in (1, -1))
        peers2 = tuple({axis2: turn(me2, d, n2)} for d in (1, -1))
        plans.append((index, src, full, block, n1, n2, sem1, sem2, cuts, peers1, peers2))

    def off(k):
        odd = lax.rem(k, 2)
        return (1 - odd) * (k // 2) - odd * ((k + 1) // 2)

    def first_stage(plan, t):
        index, src, full, block, n1, n2, sem1, sem2, cuts, peers1, peers2 = plan
        send = sends.at[3 * index]

        @pl.when(t == 0)
        def _():
            mine = full.at[block(0, 0)]
            for d in range(2):
                remote(src, mine, send, sem1.at[1 + d], peers1[d]).start()
            for d in range(2):
                remote(src, mine, send, sem2.at[d, 0, 0], peers2[d]).start()

        @pl.when((t > 0) & (t < n1))
        def _():
            at = full.at[block(off(t), 0)]
            remote(at, at, send, sem1.at[t], peers1[0]).wait_recv()
            odd = lax.rem(t, 2)

            @pl.when((odd == 1) & (t < n1 - 1))
            def _():
                remote(at, at, send, sem1.at[t + 2], peers1[0]).start()

            @pl.when((odd == 0) & (t < n1 - 2))
            def _():
                remote(at, at, send, sem1.at[t + 2], peers1[1]).start()

            for d in range(2):
                remote(at, at, send, sem2.at[d, 0, t], peers2[d]).start()

    def later_stage(plan, t, h):
        index, src, full, block, n1, n2, sem1, sem2, cuts, peers1, peers2 = plan
        last = n2 // 2
        k = t - 2 * h

        @pl.when((k >= 0) & (k < n1))
        def _():
            for d in range(2):
                at = full.at[block(off(k), -h if d == 0 else h)]
                if h == last:
                    part = at.at[:, cuts[d]]
                    remote(
                        part, part, sends.at[3 * index + 1 + d], sem2.at[d, h - 1, k], peers2[d]
                    ).wait_recv()
                    continue
                remote(at, at, sends.at[3 * index], sem2.at[d, h - 1, k], peers2[d]).wait_recv()
                if h + 1 == last:
                    part = at.at[:, cuts[d]]
                    remote(
                        part, part, sends.at[3 * index + 1 + d], sem2.at[d, h, k], peers2[d]
                    ).start()
                else:
                    remote(at, at, sends.at[3 * index], sem2.at[d, h, k], peers2[d]).start()

    def tick(t, carry):
        for plan in plans:
            first_stage(plan, t)
        for h in range(1, max(NX, NZ) // 2 + 1):
            for plan in plans:
                if h <= plan[5] // 2:
                    later_stage(plan, t, h)
        return carry

    lax.fori_loop(0, NX + NZ, tick, 0)
    for copy in own:
        copy.wait()
    for index, src, full, block, n1, n2, sem1, sem2, cuts, peers1, peers2 in plans:
        count = (n1 - 1) + 2 * n1 * (n2 // 2 - 1)
        whole = full.at[pl.ds(0, count)]
        remote(whole, whole, sends.at[3 * index], sem1.at[0], peers1[0]).wait_send()
        for d in range(2):
            part = full.at[pl.ds(0, n1), :, cuts[d]]
            remote(part, part, sends.at[3 * index + 1 + d], sem1.at[0], peers1[0]).wait_send()


def gather_all(a, b):
    n = NX * NZ
    dma = pltpu.SemaphoreType.DMA
    return pl.pallas_call(
        gather_kernel,
        out_shape=(
            jax.ShapeDtypeStruct((n, *a.shape), a.dtype),
            jax.ShapeDtypeStruct((n, *b.shape), b.dtype),
        ),
        in_specs=[pl.BlockSpec(memory_space=pltpu.VMEM)] * 2,
        out_specs=(pl.BlockSpec(memory_space=pl.ANY),) * 2,
        scratch_shapes=[
            dma((NZ,)),
            dma((2, NX // 2, NZ)),
            dma((NX,)),
            dma((2, NZ // 2, NX)),
            dma((6,)),
            dma((2,)),
        ],
        compiler_params=pltpu.CompilerParams(collective_id=1, has_side_effects=True),
        name="gather_weights",
    )(a, b)


def embed_kernel(part, out, got1, s2, got2, s3, got3, send, r1, r2, r3, core_sem):
    x, z, n = lax.axis_index(X), lax.axis_index(Z), lax.axis_index(CORE)
    greet(others(X, NX) + others(Z, NZ) + [{CORE: 1 - n}])
    copies = []
    for d in range(1, NZ):
        to = turn(z, d, NZ)
        copy = remote(part.at[to], got1.at[d], send.at[d], r1.at[d], {Z: to})
        copy.start()
        copies.append(copy)
    total = part[z].astype(jnp.float32)
    for d, copy in enumerate(copies, 1):
        copy.wait_recv()
        total = total + got1[d].astype(jnp.float32)
    for copy in copies:
        copy.wait_send()
    for q in range(QUEST):
        s2[q] = total[2 * q : 2 * q + 2]
    copies = []
    for d in range(1, NX):
        to = turn(x, d, NX)
        copy = remote(s2.at[to // 2], got2.at[d], send.at[d], r2.at[d], {X: to})
        copy.start()
        copies.append(copy)
    total = s2[x // 2]
    for d, copy in enumerate(copies, 1):
        copy.wait_recv()
        total = total + got2[d]
    for copy in copies:
        copy.wait_send()
    s3[...] = total
    got3[z] = total
    copies = []
    for d in range(1, NZ):
        copy = remote(s3, got3.at[z], send.at[d], r3.at[d], {Z: turn(z, d, NZ)})
        copy.start()
        copies.append(copy)
    for d in range(1, NZ):
        slot = got3.at[turn(z, -d, NZ)]
        remote(slot, slot, send.at[d], r3.at[d], {Z: turn(z, d, NZ)}).wait_recv()
    for copy in copies:
        copy.wait_send()
    copy = remote(got3, out.at[n], send.at[0], core_sem.at[0], {CORE: 1 - n})
    copy.start()
    out[n] = got3[...]
    other = out.at[1 - n]
    remote(other, other, send.at[0], core_sem.at[0], {CORE: 1 - n}).wait_recv()
    copy.wait_send()


def embed_rows(part):
    dma = pltpu.SemaphoreType.DMA
    half = part.shape[2]
    return pl.pallas_call(
        embed_kernel,
        out_shape=jax.ShapeDtypeStruct((2, NZ, 2, half), jnp.float32),
        in_specs=[pl.BlockSpec(memory_space=pltpu.VMEM)],
        out_specs=pl.BlockSpec(memory_space=pltpu.VMEM),
        scratch_shapes=[
            pltpu.VMEM(part.shape, part.dtype),
            pltpu.VMEM((QUEST, 2, half), jnp.float32),
            pltpu.VMEM((NX, 2, half), jnp.float32),
            pltpu.VMEM((2, half), jnp.float32),
            pltpu.VMEM((NZ, 2, half), jnp.float32),
            dma((NZ,)),
            dma((NZ,)),
            dma((NX,)),
            dma((NZ,)),
            dma((1,)),
        ],
        compiler_params=pltpu.CompilerParams(collective_id=2, has_side_effects=True),
        name="embed_rows",
    )(part)


def join(parts):
    top = functools.reduce(jnp.maximum, [lse for _, lse in parts])
    weight, total = 0.0, 0.0
    for value, lse in parts:
        factor = jnp.exp(lse - top)
        weight = weight + factor
        total = total + factor * value
    return total / weight, top + jnp.log(weight)


def finish_kernel(
    part, emb, out_w, out, got1, s2, got2, s3, got3, wide, s4, got4, send, r1, r2, r3, r4, r5
):
    x, z, n = lax.axis_index(X), lax.axis_index(Z), lax.axis_index(CORE)
    mate = x + 1 - 2 * lax.rem(x, 2)
    greet(others(Z, NZ) + others(X, NX, (2, 4, 6)) + [{X: mate}, {CORE: 1 - n}])
    copies = []
    for d in range(1, NZ):
        to = turn(z, d, NZ)
        copy = remote(part.at[to], got1.at[d], send.at[d], r1.at[d], {Z: to})
        copy.start()
        copies.append(copy)
    parts = [(part[z, 0], part[z, 1])]
    for d, copy in enumerate(copies, 1):
        copy.wait_recv()
        parts.append((got1[d, 0], got1[d, 1]))
    for copy in copies:
        copy.wait_send()
    value, lse = join(parts)
    s2[0] = value
    s2[1] = lse
    copy = remote(s2, got2, send.at[0], r2.at[0], {X: mate})
    copy.start()
    copy.wait()
    value, _ = join([(value, lse), (got2[0], got2[1])])
    wide[...] = value
    slices = value.shape[0] // 2
    summed = 0.0
    for r in range(slices):
        lhs = wide[2 * r : 2 * r + 2].astype(jnp.bfloat16)
        summed = summed + lax.dot_general(
            lhs,
            out_w[:, 128 * r : 128 * (r + 1)],
            (((1,), (1,)), ((), ())),
            preferred_element_type=jnp.float32,
        )
    half = summed.shape[1] // 2
    s3[0] = summed[:, :half]
    s3[1] = summed[:, half:]
    copy = remote(s3.at[1 - n], got3, send.at[0], r3.at[0], {CORE: 1 - n})
    copy.start()
    copy.wait()
    result = emb[n, z] + (s3[n] + got3[...])
    for r in range(slices):
        wide[2 * r : 2 * r + 2] = result[:, 128 * r : 128 * (r + 1)]
    rows = wide[...].astype(jnp.bfloat16)
    s4[...] = rows
    got4[x // 2] = rows
    copies = []
    for d in (2, 4, 6):
        copy = remote(s4, got4.at[x // 2], send.at[d], r4.at[d], {X: turn(x, d, NX)})
        copy.start()
        copies.append(copy)
    for d in (2, 4, 6):
        slot = got4.at[turn(x, -d, NX) // 2]
        remote(slot, slot, send.at[d], r4.at[d], {X: turn(x, d, NX)}).wait_recv()
    for copy in copies:
        copy.wait_send()
    copies = []
    for d in range(1, NZ):
        copy = remote(got4, out.at[z], send.at[d], r5.at[d], {Z: turn(z, d, NZ)})
        copy.start()
        copies.append(copy)
    out[z] = got4[...]
    for d in range(1, NZ):
        slot = out.at[turn(z, -d, NZ)]
        remote(slot, slot, send.at[d], r5.at[d], {Z: turn(z, d, NZ)}).wait_recv()
    for copy in copies:
        copy.wait_send()


def finish(part, emb, out_w):
    dma = pltpu.SemaphoreType.DMA
    f32 = jnp.float32
    half = emb.shape[3]
    return pl.pallas_call(
        finish_kernel,
        out_shape=jax.ShapeDtypeStruct((NZ, QUEST, 8, 128), jnp.bfloat16),
        in_specs=[pl.BlockSpec(memory_space=pltpu.VMEM)] * 3,
        out_specs=pl.BlockSpec(memory_space=pltpu.VMEM),
        scratch_shapes=[
            pltpu.VMEM(part.shape, f32),
            pltpu.VMEM(part.shape[1:], f32),
            pltpu.VMEM(part.shape[1:], f32),
            pltpu.VMEM((2, 2, half), f32),
            pltpu.VMEM((2, half), f32),
            pltpu.VMEM((8, 128), f32),
            pltpu.VMEM((8, 128), jnp.bfloat16),
            pltpu.VMEM((QUEST, 8, 128), jnp.bfloat16),
            dma((NZ,)),
            dma((NZ,)),
            dma((1,)),
            dma((1,)),
            dma((NX,)),
            dma((NZ,)),
        ],
        compiler_params=pltpu.CompilerParams(collective_id=3, has_side_effects=True),
        name="finish",
    )(part, emb, out_w)


def over_copies(x, axis):
    copies = jnp.broadcast_to(x, (lax.axis_size(axis), *x.shape))
    return lax.all_to_all(copies, axis, split_axis=0, concat_axis=0, tiled=True).sum(axis=0)


def per_device(
    hidden_in,
    ffn_gain,
    wi_gate,
    wi_up,
    wo_down,
    final_gain,
    key_w,
    value_w,
    query_w,
    out_w,
    dec_gain,
    embed,
    lengths,
    answer_ids,
):
    rows = hidden_in.shape[0]
    f32 = jnp.float32
    answers = answer_ids.shape[1]
    vocab_rows, width = embed.shape
    half = width // 2
    ids = answer_ids.reshape(NX, NZ).T.reshape(-1) - lax.axis_index(WIDE) * vocab_rows
    onehot = (ids[:, None] == jnp.arange(vocab_rows, dtype=jnp.int32)[None, :]).astype(jnp.bfloat16)
    table = lax.dynamic_slice_in_dim(embed, lax.axis_index(CORE) * half, half, 1)
    picks = jnp.dot(onehot, table, preferred_element_type=f32).astype(jnp.bfloat16)
    emb = embed_rows(picks.reshape(NZ, NX, half))
    own = emb.transpose(2, 1, 0, 3).reshape(answers, width)
    dec_in = rms_scale(own, dec_gain).astype(jnp.bfloat16)

    ff, proj = wi_gate.shape[1], key_w.shape[1]
    a = jnp.concatenate((wo_down.T, key_w, value_w, query_w, out_w.T), axis=1)
    b = jnp.concatenate((wi_gate, wi_up), axis=1)
    fa, fb = gather_all(a, b)
    fa = fa.reshape(width, a.shape[1])
    fb = fb.reshape(width, b.shape[1])
    down_t, key_full, value_full, query_full, out_t = jnp.split(
        fa, (ff, ff + proj, ff + 2 * proj, ff + 3 * proj), axis=1
    )

    resid_in = hidden_in.astype(f32)
    enc_in = rms_scale(resid_in, ffn_gain).astype(jnp.bfloat16)
    gate = jnp.dot(enc_in, fb[:, :ff], preferred_element_type=f32)
    up = jnp.dot(enc_in, fb[:, ff:], preferred_element_type=f32)
    inner = (jax.nn.gelu(gate, approximate=True) * up).astype(jnp.bfloat16)
    partial_down = lax.dot_general(
        inner, down_t, (((1,), (1,)), ((), ())), preferred_element_type=f32
    )
    resid = resid_in + over_copies(partial_down, CORE)
    memory = rms_scale(resid, final_gain).astype(jnp.bfloat16)

    keys = jnp.dot(memory, key_full, preferred_element_type=f32).astype(jnp.bfloat16)
    values = jnp.dot(memory, value_full, preferred_element_type=f32).astype(jnp.bfloat16)
    query = jnp.dot(dec_in, query_full, preferred_element_type=f32).astype(jnp.bfloat16)
    heads_local = proj // HEAD_DIM
    query_three = query.reshape(answers, heads_local, HEAD_DIM)
    keys_three = keys.reshape(rows, heads_local, HEAD_DIM)
    values_three = values.reshape(rows, heads_local, HEAD_DIM).astype(f32)
    scores = jnp.einsum(
        "ahd,khd->ahk", query_three, keys_three, preferred_element_type=f32
    ) * (1.0 / math.sqrt(HEAD_DIM))
    pass_dev = lengths.shape[0]
    passage_len = rows // pass_dev
    live = (jnp.arange(passage_len, dtype=jnp.int32)[None, :] < lengths[:, None]).reshape(rows)
    scores = jnp.where(live[None, None, :], scores, FLOOR)
    top = jnp.max(scores, axis=2)
    weights = jnp.exp(scores - top[:, :, None])
    total = jnp.sum(weights, axis=2)
    acc = jnp.einsum("ahk,khd->ahd", weights, values_three) / total[:, :, None]
    lse = jnp.broadcast_to((top + jnp.log(total))[:, :, None], acc.shape)
    both = jnp.stack((acc.reshape(answers, proj), lse.reshape(answers, proj)))
    both = both.reshape(2, 2, NZ, proj // 128, 128).transpose(2, 0, 3, 1, 4)
    rows_out = finish(both.reshape(NZ, 2, -1, 128), emb, out_t)
    rows_out = rows_out.reshape(NZ, QUEST, -1, 2, 128).transpose(1, 3, 0, 2, 4)
    return memory, rows_out.reshape(QUEST * answers, half)


def solution(mesh):
    torus = Mesh(
        mesh.devices.reshape(mesh.shape["groups"], NX, NZ, mesh.shape["narrow"]),
        ("groups", "wide_0", "wide_1", "narrow"),
    )
    return jax.shard_map(
        per_device,
        mesh=torus,
        in_specs=(
            P(GROUPS_WIDE, None),
            P(),
            P(WIDE, "narrow"),
            P(WIDE, "narrow"),
            P("narrow", WIDE),
            P(),
            P(WIDE, "narrow"),
            P(WIDE, "narrow"),
            P(WIDE, "narrow"),
            P("narrow", WIDE),
            P(),
            P(WIDE, None),
            P(GROUPS_WIDE),
            P("groups", None),
        ),
        out_specs=(P(GROUPS_WIDE, None), P("groups", "narrow")),
        check_vma=False,
    )
```

time: 732 us -> 246 us (0.34)
  waiting for transfers between devices: 540 us -> 3.54 us
  Pallas kernels: 0 us -> 191 us
  blocking collectives: 72.5 us -> 0 us
  local copies, waits for them, and re-layouts: 65.7 us -> 13 us
  between operations: 16.3 us -> 0.9 us
  other arithmetic: 17 us -> 7.93 us
  starting transfers between devices: 0.64 us -> 9.51 us
    psum x1 -> x0, waiting for transfers between devices: 277 us -> none  [per_device(): lax.psum(jnp.dot(onehot, embed, preferred_element_type=jnp.float32), WIDE)]
    all_gather x6 -> x0, waiting for transfers between devices: 262 us -> none  [the longest x2 111 us: in_one_piece(): lax.all_gather(both, axis, axis=dim, tiled=True)]
    pallas_call x0 -> x3, Pallas kernels: none -> 191 us  [the longest x1 122 us: gather_all(): pl.pallas_call(gather_kernel, out_shape=(jax.ShapeDtypeStruct((n, *a.shap...]
    all_gather x2 -> x0, blocking collectives: 44.4 us -> none  [all_blocks(): tiles = lax.all_gather(tiles, axes[k])]
    all_to_all x2 -> x0, blocking collectives: 28.1 us -> none  [the longest x1 15.5 us: from_everyone(): return lax.all_to_all(copies, axis, split_axis=0, concat_axis=0, tiled=True)]
    unnamed x47 -> x23, local copies, waits for them, and re-layouts: 27.5 us -> 3.72 us
    squeeze x80 -> x0, local copies, waits for them, and re-layouts: 20.1 us -> none  [the longest x74 18.4 us: joined_all(): x = combine(x, jax.tree.map(lambda part: part[k], pieces))]
    slice x5 -> x0, local copies, waits for them, and re-layouts: 10.3 us -> none  [the longest x2 6.4 us: joined_all(): x = jax.tree.map(lambda part: part[0], pieces)]
  transfers between devices with their start and end apart: 7 -> 1, of which waited for: 5 -> 1; matrix products, arithmetic and copies ran while one was open for 4% -> 0% of each run, Pallas kernels for 0% -> 0%
where the time goes in v1:
time: 246 us; the launch traced here: 245 us
  Pallas kernels  191 us (78%)
  matrix products  18.4 us (7%)
  local copies, waits for them, and re-layouts  13 us (5%)
  starting transfers between devices  9.51 us (4%)
  other arithmetic  7.93 us (3%)
  waiting for transfers between devices  3.54 us (1%)
    pallas_call x1, Pallas kernels, gather_all(): pl.pallas_call(gather_kernel, out_shape=(jax.ShapeDtypeStruct((n, *a.shap...  122 us
    pallas_call x1, Pallas kernels, finish(): pl.pallas_call(finish_kernel, out_shape=jax.ShapeDtypeStruct((NZ, QUEST,...  36.5 us
    pallas_call x1, Pallas kernels, embed_rows(): pl.pallas_call(embed_kernel, out_shape=jax.ShapeDtypeStruct((2, NZ, 2, ha...  32.6 us
    all_to_all x1, starting transfers between devices, over_copies(): lax.all_to_all(copies, axis, split_axis=0, concat_axis=0, tiled=True)  9.51 us
    dot_general x1, matrix products, per_device(): lax.dot_general(inner, down_t, (((1,), (1,)), ((), ())), preferred_elemen...  6.13 us
    dot_general x1, matrix products, per_device(): gate = jnp.dot(enc_in, fb[:, :ff], preferred_element_type=f32)  5.29 us
  transfers between devices with their start and end apart: 1, of which 1 were waited for; matrix products, arithmetic and copies ran while one was open for 0% of the time, Pallas kernels for 0%

profile of v1, /device:TPU:65, one launch (start us, length us, event | category | flops | bytes accessed | tf_op | source)
XLA Modules:
  0.0 244.6 jit_solution(12246319361737208504)
XLA Ops:
  0.6 0.8 bitcast_dynamic-update-slice_fusion
  1.4 0.7 convert_element_type.39
  2.1 1.4 fusion.17
  3.5 0.7 constant_dynamic-update-slice_fusion.3
  4.2 0.7 constant_dynamic-update-slice_fusion.2
  4.9 0.7 constant_dynamic-update-slice_fusion.1
  5.6 0.7 constant_dynamic-update-slice_fusion.a_ref
  6.3 1.4 pad_maximum_fusion.b_ref
  7.7 122.3 %gather_weights.1 = (bf16[128,8,3456]{2,1,0:T(8,128)(2,1)}, bf16[128,8,2816]{2,1,0:T(8,128)(2,1)}) custom-call(bf16[8,3456]{1,0:T(8,128)(2,1)} %copy-done.3, bf16[8,2816]{1,0:T(8,128)(2,1)} %pad_maximum_fusion.b_ref), custom_call_target="tpu_custom_call" | custom-call | tf_op jit(solution)/shard_map/gather_weights/pallas_call | solution.py:160
  130.0 5.3 %fusion.14 = f32[400,1408]{1,0:T(8,128)} fusion(bf16[1024,2816]{1,0:T(8,128)(2,1)} %bitcast.52, bf16[400,1024]{1,0:T(8,128)(2,1)} %param.14, f32[1024]{0:T(1024)S(1)} %convert_element_type.39, f32[400]{0:T(512)S(1)} %add_rsqrt_fusion.2), kind=kOutput, calls=%fused_computation.17 | convolution fusion | flops 1159577600 | bytes 5961280 | tf_op jit(solution)/shard_map/dot_general | solution.py:412
  135.3 6.1 %fusion = f32[400,1024]{1,0:T(8,128)S(1)} fusion(bf16[1024,3456]{1,0:T(8,128)(2,1)} %bitcast.39, f32[400,1408]{1,0:T(8,128)} %fusion.14, bf16[1024,2816]{1,0:T(8,128)(2,1)} %bitcast.53, bf16[400,1024]{1,0:T(8,128)(2,1)S(1)} %copy-done.1, f32[1024]{0:T(1024)S(1)} %convert_element_type.39, f32[400]{0:T(512)S(1)} %add_rsqrt_fusion.2), kind=kOutput, calls=%fused_computation.2 | convolution fusion | flops 2309632000 | bytes 10483264 | tf_op jit(solution)/shard_map/dot_general | solution.py:415
  141.4 2.2 broadcast_in_dim.12
  143.7 9.5 %all-to-all-start = ((f32[2,400,1024]{2,1,0:T(8,128)}), f32[2,400,1024]{2,1,0:T(8,128)}, u32[]{:S(2)}, u32[]{:S(2)}) async-start(f32[2,400,1024]{2,1,0:T(8,128)} %broadcast_in_dim.12), calls=%async_computation | async-start | bytes 6553600 | tf_op jit(solution)/shard_map/all_to_all | solution.py:368
  153.2 3.5 %all-to-all-done = f32[2,400,1024]{2,1,0:T(8,128)} async-done(((f32[2,400,1024]{2,1,0:T(8,128)}), f32[2,400,1024]{2,1,0:T(8,128)}, u32[]{:S(2)}, u32[]{:S(2)}) %all-to-all-start) | async-done | bytes 3276832 | tf_op jit(solution)/shard_map/all_to_all | solution.py:368
  156.7 2.4 reduce_sum.46
  159.2 0.3 multiply_reduce_fusion
  159.5 0.3 multiply_convert_fusion
  159.8 2.1 convolution_convert_fusion
  161.9 1.8 convolution_convert_fusion.1
  163.8 2.3 split.24.out_w
  166.6 0.9 fusion.23.part
  167.4 32.6 %embed_rows.1.emb = f32[2,16,2,512]{3,2,1,0:T(2,128)} custom-call(bf16[16,8,512]{2,1,0:T(8,128)(2,1)} %fusion.23.part), custom_call_target="tpu_custom_call" | custom-call | tf_op jit(solution)/shard_map/embed_rows/pallas_call | solution.py:233
  200.0 1.0 multiply_reduce_fusion.1
  201.1 1.0 copy.54
  202.3 1.5 convolution_convert_fusion.3
  204.1 0.3 fusion.40
  204.4 0.2 fusion.29
  205.2 0.3 fusion.22
  205.7 0.8 copy.59
  206.5 36.5 %finish.1 = bf16[16,4,8,128]{3,2,1,0:T(8,128)(2,1)} custom-call(f32[16,2,8,128]{3,2,1,0:T(8,128)} %bitcast.48, f32[2,16,2,512]{3,2,1,0:T(2,128)} %embed_rows.1.emb, bf16[1024,512]{1,0:T(8,128)(2,1)} %split.24.out_w), custom_call_target="tpu_custom_call" | custom-call | tf_op jit(solution)/shard_map/finish/pallas_call | solution.py:340
  243.0 0.9 copy.60
  243.9 0.7 copy.69
  (40 shorter events, 1.7 us)
Async XLA Ops:
  0.6 165.9 %copy-start = (bf16[251,1024]{1,0:T(8,128)(2,1)S(1)}, bf16[251,1024]{1,0:T(8,128)(2,1)}, u32[]{:S(2)}) copy-start(bf16[251,1024]{1,0:T(8,128)(2,1)} %param.25) | copy-start | bytes 1542148
  6.3 1.4 copy-start.3
  130.0 5.3 %copy-start.1 = (bf16[400,1024]{1,0:T(8,128)(2,1)S(1)}, bf16[400,1024]{1,0:T(8,128)(2,1)}, u32[]{:S(2)}) copy-start(bf16[400,1024]{1,0:T(8,128)(2,1)} %param.14) | copy-start | bytes 2457604
  143.7 9.5 %copy-start.4 = (bf16[1024]{0:T(1024)(128)(2,1)S(1)}, bf16[1024]{0:T(1024)(128)(2,1)}, u32[]{:S(2)}) copy-start(bf16[1024]{0:T(1024)(128)(2,1)} %param.19) | copy-start | bytes 6148
  143.7 13.1 %all-to-all-start = ((f32[2,400,1024]{2,1,0:T(8,128)}), f32[2,400,1024]{2,1,0:T(8,128)}, u32[]{:S(2)}, u32[]{:S(2)}) async-start(f32[2,400,1024]{2,1,0:T(8,128)} %broadcast_in_dim.12), calls=%async_computation | async-start | bytes 6553600 | tf_op jit(solution)/shard_map/all_to_all | solution.py:368
  159.8 4.0 %copy-start.2 = (bf16[400,1024]{1,0:T(8,128)(2,1)}, bf16[400,1024]{1,0:T(8,128)(2,1)S(1)}, u32[]{:S(2)}) copy-start(bf16[400,1024]{1,0:T(8,128)(2,1)S(1)} %multiply_convert_fusion) | copy-start | bytes 2457604
  163.8 2.5 %copy-start.6 = (s32[4,32]{1,0:T(4,128)S(1)}, s32[4,32]{1,0:T(4,128)}, u32[]{:S(2)}) copy-start(s32[4,32]{1,0:T(4,128)} %param.27) | copy-start | bytes 1540
  163.8 38.3 %copy-start.5 = (bf16[1024]{0:T(1024)(128)(2,1)S(1)}, bf16[1024]{0:T(1024)(128)(2,1)}, u32[]{:S(2)}) copy-start(bf16[1024]{0:T(1024)(128)(2,1)} %param.24) | copy-start | bytes 6148
  166.1 37.9 %copy-start.7 = (s32[2]{0:T(128)S(1)}, s32[2]{0:T(128)}, u32[]{:S(2)}) copy-start(s32[2]{0:T(128)} %param.26) | copy-start | bytes 28

commit v2 on v1

v2 whole, which is shorter than its diff:
```python
import functools
import math

import jax
import jax.numpy as jnp
from jax import lax
from jax.experimental import pallas as pl
from jax.experimental.pallas import tpu as pltpu
from jax.sharding import Mesh
from jax.sharding import PartitionSpec as P

HEAD_DIM = 64
QUEST = 4
WIDE = ("wide_0", "wide_1")
GROUPS_WIDE = ("groups", "wide_0", "wide_1")
X, Z, CORE = "wide_0", "wide_1", "narrow"
NX, NZ = 8, 16
MESH = pl.DeviceIdType.MESH

EPS = 1e-06
FLOOR = -1e30


def turn(i, by, n):
    return lax.rem(i + (by + 2 * n), n)


def others(axis, n, steps=None):
    me = lax.axis_index(axis)
    return [{axis: turn(me, d, n)} for d in (steps or range(1, n))]


def remote(src, dst, send, recv, peer):
    return pltpu.make_async_remote_copy(
        src_ref=src, dst_ref=dst, send_sem=send, recv_sem=recv, device_id=peer, device_id_type=MESH
    )


def join(parts):
    top = functools.reduce(jnp.maximum, [lse for _, lse in parts])
    weight, total = 0.0, 0.0
    for value, lse in parts:
        factor = jnp.exp(lse - top)
        weight = weight + factor
        total = total + factor * value
    return total / weight, top + jnp.log(weight)


def dot(a, b, transposed=False):
    return lax.dot_general(
        a, b, (((1,), (1 if transposed else 0,)), ((), ())), preferred_element_type=jnp.float32
    )


def rows_of(index, count):
    return pl.ds(pl.multiple_of(index * count, count), count)


def reader_kernel(
    hidden,
    gains,
    gate_w,
    up_w,
    down_w,
    key_w,
    value_w,
    query_w,
    out_w,
    table,
    ids,
    lengths,
    memory,
    decoded,
    a_own,
    b_own,
    fa,
    fb,
    enc,
    inner,
    down_mine,
    down_other,
    picks,
    e1,
    e2_src,
    e2,
    e3_src,
    e3,
    emb,
    own_rows,
    part,
    f1,
    f2_src,
    f2,
    wide,
    f3_src,
    f3,
    f4_src,
    f4,
    f5,
    flat,
    a1,
    a2,
    b1,
    b2,
    sends,
    down_send,
    down_recv,
    e_send,
    e_r1,
    e_r2,
    e_r3,
    e_r4,
    f_send,
    f_r1,
    f_r2,
    f_r3,
    f_r4,
    f_r5,
):
    f32, bf16 = jnp.float32, jnp.bfloat16
    x, z, n = lax.axis_index(X), lax.axis_index(Z), lax.axis_index(CORE)
    core = {CORE: 1 - n}
    mate = x + 1 - 2 * lax.rem(x, 2)
    peers = others(X, NX) + others(Z, NZ) + [core]
    barrier = pltpu.get_barrier_semaphore()
    for peer in peers:
        pl.semaphore_signal(barrier, inc=1, device_id=peer, device_id_type=MESH)

    ff, proj = gate_w.shape[1], key_w.shape[1]
    width = hidden.shape[1]
    half = width // 2
    rows = hidden.shape[0]
    answers = own_rows.shape[0]
    at = 0
    for ref in (down_w, key_w, value_w, query_w, out_w):
        a_own[:, at : at + ref.shape[1]] = ref[...]
        at += ref.shape[1]
    for c in range(ff // 128):
        b_own[:, 256 * c : 256 * c + 128] = gate_w[:, 128 * c : 128 * (c + 1)]
        b_own[:, 256 * c + 128 : 256 * (c + 1)] = up_w[:, 128 * c : 128 * (c + 1)]

    vocab_rows = table.shape[0]
    local_ids = ids[...] - (x * NZ + z) * vocab_rows
    spot = lax.broadcasted_iota(jnp.int32, (vocab_rows, ids.shape[1]), 0)
    onehot = (spot == local_ids).astype(f32).astype(bf16)
    shares = lax.dot_general(
        onehot,
        table[:, rows_of(n, half)],
        (((0,), (0,)), ((), ())),
        preferred_element_type=f32,
    ).astype(bf16)
    for k in range(NZ):
        picks[k] = shares[NX * k : NX * (k + 1)]
    pl.semaphore_wait(barrier, len(peers))

    def block_a(first, second):
        return turn(x, second, NX) * NZ + turn(z, first, NZ)

    def block_b(first, second):
        return turn(x, first, NX) * NZ + turn(z, second, NZ)

    plans = []
    for index, (src, full, block, axis1, n1, axis2, n2, sem1, sem2) in enumerate(
        ((a_own, fa, block_a, Z, NZ, X, NX, a1, a2), (b_own, fb, block_b, X, NX, Z, NZ, b1, b2))
    ):
        columns = src.shape[1]
        middle = columns // 256 * 128
        cuts = (pl.ds(0, middle), pl.ds(middle, columns - middle))
        me1, me2 = lax.axis_index(axis1), lax.axis_index(axis2)
        peers1 = tuple({axis1: turn(me1, d, n1)} for d in (1, -1))
        peers2 = tuple({axis2: turn(me2, d, n2)} for d in (1, -1))
        plans.append((index, src, full, block, n1, n2, sem1, sem2, cuts, peers1, peers2))

    def off(k):
        odd = lax.rem(k, 2)
        return (1 - odd) * (k // 2) - odd * ((k + 1) // 2)

    def first_stage(plan, t):
        index, src, full, block, n1, n2, sem1, sem2, cuts, peers1, peers2 = plan
        send = sends.at[3 * index]

        @pl.when(t == 0)
        def _():
            mine = full.at[block(0, 0)]
            for d in range(2):
                remote(src, mine, send, sem1.at[1 + d], peers1[d]).start()
            for d in range(2):
                remote(src, mine, send, sem2.at[d, 0, 0], peers2[d]).start()

        @pl.when((t > 0) & (t < n1))
        def _():
            at = full.at[block(off(t), 0)]
            remote(at, at, send, sem1.at[t], peers1[0]).wait_recv()
            odd = lax.rem(t, 2)

            @pl.when((odd == 1) & (t < n1 - 1))
            def _():
                remote(at, at, send, sem1.at[t + 2], peers1[0]).start()

            @pl.when((odd == 0) & (t < n1 - 2))
            def _():
                remote(at, at, send, sem1.at[t + 2], peers1[1]).start()

            for d in range(2):
                remote(at, at, send, sem2.at[d, 0, t], peers2[d]).start()

    def later_stage(plan, t, h):
        index, src, full, block, n1, n2, sem1, sem2, cuts, peers1, peers2 = plan
        last = n2 // 2
        k = t - 2 * h

        @pl.when((k >= 0) & (k < n1))
        def _():
            for d in range(2):
                at = full.at[block(off(k), -h if d == 0 else h)]
                if h == last:
                    part = at.at[:, cuts[d]]
                    remote(
                        part, part, sends.at[3 * index + 1 + d], sem2.at[d, h - 1, k], peers2[d]
                    ).wait_recv()
                    continue
                remote(at, at, sends.at[3 * index], sem2.at[d, h - 1, k], peers2[d]).wait_recv()
                if h + 1 == last:
                    part = at.at[:, cuts[d]]
                    remote(
                        part, part, sends.at[3 * index + 1 + d], sem2.at[d, h, k], peers2[d]
                    ).start()
                else:
                    remote(at, at, sends.at[3 * index], sem2.at[d, h, k], peers2[d]).start()

    def tick(t, carry):
        for plan in plans:
            first_stage(plan, t)
        for h in range(1, max(NX, NZ) // 2 + 1):
            for plan in plans:
                if h <= plan[5] // 2:
                    later_stage(plan, t, h)
        return carry

    first_copies = []
    for d in range(1, NZ):
        to = turn(z, d, NZ)
        copy = remote(picks.at[to], e1.at[d], e_send.at[d], e_r1.at[d], {Z: to})
        copy.start()
        first_copies.append(copy)
    lax.fori_loop(0, 2, tick, 0)

    resid_in = hidden[...].astype(f32)
    mean_square = jnp.mean(resid_in * resid_in, axis=-1, keepdims=True)
    enc[...] = (resid_in * lax.rsqrt(mean_square + EPS) * gains[0:1]).astype(bf16)
    fa[x * NZ + z] = a_own[...]
    fb[x * NZ + z] = b_own[...]
    lax.fori_loop(2, 5, tick, 0)

    total = picks[z].astype(f32)
    for d, copy in enumerate(first_copies, 1):
        copy.wait_recv()
        total = total + e1[d].astype(f32)
    for copy in first_copies:
        copy.wait_send()
    for q in range(QUEST):
        for r in range(half // 128):
            e2_src[q, 2 * r : 2 * r + 2] = total[2 * q : 2 * q + 2, 128 * r : 128 * (r + 1)]
    copies = []
    for d in range(1, NX):
        to = turn(x, d, NX)
        copy = remote(e2_src.at[to // 2], e2.at[d], e_send.at[d], e_r2.at[d], {X: to})
        copy.start()
        copies.append(copy)
    lax.fori_loop(5, 8, tick, 0)

    total = e2_src[x // 2]
    for d, copy in enumerate(copies, 1):
        copy.wait_recv()
        total = total + e2[d]
    for copy in copies:
        copy.wait_send()
    e3_src[...] = total
    e3[rows_of(z, 8)] = total
    copies = []
    for d in range(1, NZ):
        copy = remote(
            e3_src, e3.at[rows_of(z, 8)], e_send.at[d], e_r3.at[d], {Z: turn(z, d, NZ)}
        )
        copy.start()
        copies.append(copy)
    lax.fori_loop(8, 12, tick, 0)

    for d in range(1, NZ):
        slot = e3.at[rows_of(turn(z, -d, NZ), 8)]
        remote(slot, slot, e_send.at[d], e_r3.at[d], {Z: turn(z, d, NZ)}).wait_recv()
    for copy in copies:
        copy.wait_send()
    copy = remote(e3, emb.at[rows_of(n, 8 * NZ)], e_send.at[0], e_r4.at[0], core)
    copy.start()
    emb[rows_of(n, 8 * NZ)] = e3[...]
    lax.fori_loop(12, 16, tick, 0)

    slot = emb.at[rows_of(1 - n, 8 * NZ)]
    remote(slot, slot, e_send.at[0], e_r4.at[0], core).wait_recv()
    copy.wait_send()
    for h in range(2):
        for r in range(half // 128):
            for i in range(2):
                own_rows[NZ * i : NZ * (i + 1), half * h + 128 * r : half * h + 128 * (r + 1)] = (
                    emb[pl.ds(8 * NZ * h + 2 * r + i, NZ, stride=8), :]
                )
    embedded = own_rows[...]
    mean_square = jnp.mean(embedded * embedded, axis=-1, keepdims=True)
    dec_in = (embedded * lax.rsqrt(mean_square + EPS) * gains[2:3]).astype(bf16)
    lax.fori_loop(16, NX + NZ, tick, 0)

    for index, src, full, block, n1, n2, sem1, sem2, cuts, peers1, peers2 in plans:
        count = (n1 - 1) + 2 * n1 * (n2 // 2 - 1)
        whole = full.at[pl.ds(0, count)]
        remote(whole, whole, sends.at[3 * index], sem1.at[0], peers1[0]).wait_send()
        for d in range(2):
            piece = full.at[pl.ds(0, n1), :, cuts[d]]
            remote(piece, piece, sends.at[3 * index + 1 + d], sem1.at[0], peers1[0]).wait_send()

    def ffn(c, carry):
        weight = fb[:, :, rows_of(c, 256)].reshape(width, 256)
        both = dot(enc[...], weight)
        value = jax.nn.gelu(both[:, :128], approximate=True) * both[:, 128:]
        inner[:, rows_of(c, 128)] = value.astype(bf16)
        return carry

    lax.fori_loop(0, ff // 128, ffn, 0)
    copies = []
    for c in range(width // 256):
        weight = fa[32 * c : 32 * (c + 1), :, :ff].reshape(256, ff)
        down_mine[c] = dot(inner[...], weight, True)
        copy = remote(down_mine.at[c], down_other.at[c], down_send.at[c], down_recv.at[c], core)
        copy.start()
        copies.append(copy)
    query = dot(dec_in, fa[:, :, ff + 2 * proj : ff + 3 * proj].reshape(width, proj)).astype(bf16)
    squares = 0.0
    for c, copy in enumerate(copies):
        copy.wait_recv()
        resid = hidden[:, 256 * c : 256 * (c + 1)].astype(f32) + (down_mine[c] + down_other[c])
        down_other[c] = resid
        squares = squares + jnp.sum(resid * resid, axis=-1, keepdims=True)
    scale = lax.rsqrt(squares * (1.0 / width) + EPS)
    for c in range(width // 256):
        cols = slice(256 * c, 256 * (c + 1))
        memory[:, cols] = (down_other[c] * scale * gains[1:2, cols]).astype(bf16)
    for copy in copies:
        copy.wait_send()

    mem = memory[...]
    keys = dot(mem, fa[:, :, ff : ff + proj].reshape(width, proj)).astype(bf16)
    values = dot(mem, fa[:, :, ff + proj : ff + 2 * proj].reshape(width, proj)).astype(bf16)
    heads = proj // HEAD_DIM
    head_of = lax.broadcasted_iota(jnp.int32, (answers, proj), 1) // HEAD_DIM
    spread = jnp.concatenate(
        [jnp.where(head_of == h, query.astype(f32), 0.0) for h in range(heads)], axis=0
    ).astype(bf16)
    scores = dot(spread, keys, True) * (1.0 / math.sqrt(HEAD_DIM))
    position = lax.broadcasted_iota(jnp.int32, scores.shape, 1)
    passages = lengths.shape[0]
    passage_len = rows // passages
    live = None
    for p in range(passages):
        here = (position >= p * passage_len) & (position < p * passage_len + lengths[p])
        live = here if live is None else live | here
    scores = jnp.where(live, scores, FLOOR)
    top = jnp.max(scores, axis=1, keepdims=True)
    weights = jnp.exp(scores - top)
    total = jnp.sum(weights, axis=1, keepdims=True)
    acc = dot(weights.astype(bf16), values) / total
    lse = top + jnp.log(total)
    value, spread_lse = 0.0, 0.0
    for h in range(heads):
        rows_h = slice(answers * h, answers * (h + 1))
        value = value + jnp.where(head_of == h, acc[rows_h], 0.0)
        spread_lse = spread_lse + jnp.where(head_of == h, lse[rows_h], 0.0)
    for s, block_of in enumerate((value, spread_lse)):
        for r in range(proj // 128):
            for i in range(2):
                part[pl.ds(8 * s + 2 * r + i, NZ, stride=16), :] = block_of[
                    NZ * i : NZ * (i + 1), 128 * r : 128 * (r + 1)
                ]

    copies = []
    for d in range(1, NZ):
        to = turn(z, d, NZ)
        copy = remote(
            part.at[rows_of(to, 16)], f1.at[d], f_send.at[d], f_r1.at[d], {Z: to}
        )
        copy.start()
        copies.append(copy)
    mine = part[rows_of(z, 16)]
    parts = [(mine[:8], mine[8:])]
    for d, copy in enumerate(copies, 1):
        copy.wait_recv()
        parts.append((f1[d, :8], f1[d, 8:]))
    value, lse = join(parts)
    f2_src[0] = value
    f2_src[1] = lse
    pair = remote(f2_src, f2, f_send.at[0], f_r2.at[0], {X: mate})
    pair.start()
    for copy in copies:
        copy.wait_send()
    pair.wait()
    value, _ = join([(value, lse), (f2[0], f2[1])])
    wide[...] = value
    slices = proj // 128
    summed = 0.0
    for r in range(slices):
        lhs = wide[2 * r : 2 * r + 2].astype(bf16)
        at = ff + 3 * proj + 128 * r
        summed = summed + dot(lhs, fa[:, :, at : at + 128].reshape(width, 128), True)
    for h in range(2):
        for r in range(half // 128):
            at = half * h + 128 * r
            f3_src[h, 2 * r : 2 * r + 2] = summed[:, at : at + 128]
    copy = remote(f3_src.at[1 - n], f3, f_send.at[0], f_r3.at[0], core)
    copy.start()
    copy.wait()
    result = emb[pl.ds(pl.multiple_of(n * 8 * NZ + z * 8, 8), 8)] + (f3_src[n] + f3[...])
    done = result.astype(bf16)
    f4_src[...] = done
    f4[x // 2] = done
    copies = []
    for d in (2, 4, 6):
        copy = remote(f4_src, f4.at[x // 2], f_send.at[d], f_r4.at[d], {X: turn(x, d, NX)})
        copy.start()
        copies.append(copy)
    for d in (2, 4, 6):
        slot = f4.at[turn(x, -d, NX) // 2]
        remote(slot, slot, f_send.at[d], f_r4.at[d], {X: turn(x, d, NX)}).wait_recv()
    for copy in copies:
        copy.wait_send()
    copies = []
    for d in range(1, NZ):
        copy = remote(f4, f5.at[z], f_send.at[d], f_r5.at[d], {Z: turn(z, d, NZ)})
        copy.start()
        copies.append(copy)
    f5[z] = f4[...]
    for d in range(1, NZ):
        slot = f5.at[turn(z, -d, NZ)]
        remote(slot, slot, f_send.at[d], f_r5.at[d], {Z: turn(z, d, NZ)}).wait_recv()
    for k in range(NZ):
        for q in range(QUEST):
            flat[8 * (QUEST * k + q) : 8 * (QUEST * k + q + 1)] = f5[k, q].astype(f32)
    for q in range(QUEST):
        for i in range(2):
            for r in range(half // 128):
                start = NZ * (2 * q + i)
                decoded[start : start + NZ, 128 * r : 128 * (r + 1)] = flat[
                    pl.ds(8 * q + 2 * r + i, NZ, stride=8 * QUEST), :
                ].astype(bf16)
    for copy in copies:
        copy.wait_send()


def reader(hidden, gains, shards, table, ids, lengths, answers):
    gate_w, up_w, down_w, key_w, value_w, query_w, out_w = shards
    dma = pltpu.SemaphoreType.DMA
    f32, bf16 = jnp.float32, jnp.bfloat16
    blocks = NX * NZ
    rows, width = hidden.shape
    ff, proj, half = gate_w.shape[1], key_w.shape[1], width // 2
    a_width, b_width = ff + 4 * proj, 2 * ff
    chunks = width // 256
    vmem = pltpu.VMEM
    scratch = [
        vmem((8, a_width), bf16),
        vmem((8, b_width), bf16),
        vmem((blocks, 8, a_width), bf16),
        vmem((blocks, 8, b_width), bf16),
        vmem((rows, width), bf16),
        vmem((rows, ff), bf16),
        vmem((chunks, rows, 256), f32),
        vmem((chunks, rows, 256), f32),
        vmem((NZ, NX, half), bf16),
        vmem((NZ, NX, half), bf16),
        vmem((QUEST, 8, 128), f32),
        vmem((NX, 8, 128), f32),
        vmem((8, 128), f32),
        vmem((8 * NZ, 128), f32),
        vmem((16 * NZ, 128), f32),
        vmem((answers, width), f32),
        vmem((16 * NZ, 128), f32),
        vmem((NZ, 16, 128), f32),
        vmem((2, 8, 128), f32),
        vmem((2, 8, 128), f32),
        vmem((8, 128), f32),
        vmem((2, 8, 128), f32),
        vmem((8, 128), f32),
        vmem((8, 128), bf16),
        vmem((QUEST, 8, 128), bf16),
        vmem((NZ, QUEST, 8, 128), bf16),
        vmem((NZ * QUEST * 8, 128), f32),
        dma((NZ,)),
        dma((2, NX // 2, NZ)),
        dma((NX,)),
        dma((2, NZ // 2, NX)),
        dma((6,)),
        dma((chunks,)),
        dma((chunks,)),
        dma((NZ,)),
        dma((NZ,)),
        dma((NX,)),
        dma((NZ,)),
        dma((1,)),
        dma((NZ,)),
        dma((NZ,)),
        dma((1,)),
        dma((1,)),
        dma((NX,)),
        dma((NZ,)),
    ]
    return pl.pallas_call(
        reader_kernel,
        out_shape=(
            jax.ShapeDtypeStruct((rows, width), bf16),
            jax.ShapeDtypeStruct((QUEST * answers, half), bf16),
        ),
        in_specs=[pl.BlockSpec(memory_space=vmem)] * 11 + [pl.BlockSpec(memory_space=pltpu.SMEM)],
        out_specs=(pl.BlockSpec(memory_space=vmem),) * 2,
        scratch_shapes=scratch,
        compiler_params=pltpu.CompilerParams(
            collective_id=1, has_side_effects=True, vmem_limit_bytes=60 * 2**20
        ),
        name="reader",
    )(hidden, gains, *shards, table, ids, lengths)


def per_device(
    hidden_in,
    ffn_gain,
    wi_gate,
    wi_up,
    wo_down,
    final_gain,
    key_w,
    value_w,
    query_w,
    out_w,
    dec_gain,
    embed,
    lengths,
    answer_ids,
):
    gains = jnp.stack((ffn_gain, final_gain, dec_gain)).astype(jnp.float32)
    ids = answer_ids.reshape(NX, NZ).T.reshape(1, NX * NZ)
    shards = (wi_gate, wi_up, wo_down.T, key_w, value_w, query_w, out_w.T)
    return reader(hidden_in, gains, shards, embed, ids, lengths, answer_ids.shape[1])


def solution(mesh):
    torus = Mesh(
        mesh.devices.reshape(mesh.shape["groups"], NX, NZ, mesh.shape["narrow"]),
        ("groups", "wide_0", "wide_1", "narrow"),
    )
    return jax.shard_map(
        per_device,
        mesh=torus,
        in_specs=(
            P(GROUPS_WIDE, None),
            P(),
            P(WIDE, "narrow"),
            P(WIDE, "narrow"),
            P("narrow", WIDE),
            P(),
            P(WIDE, "narrow"),
            P(WIDE, "narrow"),
            P(WIDE, "narrow"),
            P("narrow", WIDE),
            P(),
            P(WIDE, None),
            P(GROUPS_WIDE),
            P("groups", None),
        ),
        out_specs=(P(GROUPS_WIDE, None), P("groups", "narrow")),
        check_vma=False,
    )
```

time: 246 us -> 183 us (0.74)
  matrix products: 18.4 us -> 0 us
  Pallas kernels: 191 us -> 176 us
  starting transfers between devices: 9.51 us -> 0 us
  local copies, waits for them, and re-layouts: 13 us -> 5.63 us
  other arithmetic: 7.93 us -> 0.62 us
  waiting for transfers between devices: 3.54 us -> 0 us
    dot_general x8 -> x0, matrix products: 18.4 us -> none  [the longest x1 6.13 us: per_device(): lax.dot_general(inner, down_t, (((1,), (1,)), ((), ())), preferred_elemen...]
    pallas_call x3 -> x1, Pallas kernels: 191 us -> 176 us  [reader(): pl.pallas_call(reader_kernel, out_shape=(jax.ShapeDtypeStruct((rows, widt...]
    all_to_all x1 -> x0, starting transfers between devices: 9.51 us -> none  [over_copies(): lax.all_to_all(copies, axis, split_axis=0, concat_axis=0, tiled=True)]
    reduce_sum x5 -> x0, other arithmetic: 5.4 us -> none  [the longest x3 2.74 us: rms_scale(): mean_square = jnp.mean(values * values, axis=-1, keepdims=True)]
    all_to_all x1 -> x0, waiting for transfers between devices: 3.54 us -> none  [over_copies(): lax.all_to_all(copies, axis, split_axis=0, concat_axis=0, tiled=True)]
    transpose x3 -> x1, local copies, waits for them, and re-layouts: 2.71 us -> 0.07 us  [per_device(): ids = answer_ids.reshape(NX, NZ).T.reshape(1, NX * NZ)]
  transfers between devices with their start and end apart: 1 -> 0, of which waited for: 1 -> 0; matrix products, arithmetic and copies ran while one was open for 0% -> 0% of each run, Pallas kernels for 0% -> 0%
where the time goes in v2:
time: 183 us
  Pallas kernels  176 us (96%)
  local copies, waits for them, and re-layouts  5.63 us (3%)
    pallas_call x1, Pallas kernels, reader(): pl.pallas_call(reader_kernel, out_shape=(jax.ShapeDtypeStruct((rows, widt...  176 us
    unnamed x12, local copies, waits for them, and re-layouts  4.87 us

profile of v2, /device:TPU:65, one launch (start us, length us, event | category | flops | bytes accessed | tf_op | source)
XLA Modules:
  0.0 182.9 jit_solution(15881269803090144143)
XLA Ops:
  0.6 0.0 copy-start.1
  0.6 0.7 copy-done.1
  1.3 0.0 copy-start.2
  1.3 0.7 copy-done.2
  2.0 0.0 copy-start.3
  2.0 0.7 copy-done.3
  2.7 0.0 copy-start.4
  2.7 0.6 maximum_convert_fusion.gains
  3.3 0.1 copy-done.4
  3.4 0.1 reshape.10
  3.4 0.1 copy.17
  3.5 0.6 reshape.11.ids
  4.1 176.0 %reader.1 = (bf16[400,1024]{1,0:T(8,128)(2,1)}, bf16[128,512]{1,0:T(8,128)(2,1)}) custom-call(bf16[400,1024]{1,0:T(8,128)(2,1)} %hidden.1, f32[3,1024]{1,0:T(4,128)} %maximum_convert_fusion.gains, bf16[8,1408]{1,0:T(8,128)(2,1)} %gate_w.1, bf16[8,1408]{1,0:T(8,128)(2,1)} %up_w.1, bf16[8,1408]{1,0:T(8,128)(2,1)} %bitcast.3, bf16[8,512]{1,0:T(8,128)(2,1)} %key_w.1, ...), custom_call_target="tpu_custom_call" | custom-call | tf_op jit(solution)/shard_map/reader/pallas_call | solution.py:514
  180.1 0.0 copy-start
  180.1 2.1 %copy.20 = bf16[400,1024]{1,0:T(8,128)(2,1)} copy(bf16[400,1024]{1,0:T(8,128)(2,1)} %get-tuple-element.4) | data formatting | bytes 1638400
  182.3 0.0 copy-done
  182.3 0.7 copy.21
  (3 shorter events, 0.0 us)
Async XLA Ops:
  0.6 0.7 copy-start.1
  1.3 0.7 copy-start.2
  2.0 0.7 copy-start.3
  2.7 0.7 copy-start.4
  180.1 2.1 %copy-start = (bf16[128,512]{1,0:T(8,128)(2,1)S(1)}, bf16[128,512]{1,0:T(8,128)(2,1)}, u32[]{:S(2)}) copy-start(bf16[128,512]{1,0:T(8,128)(2,1)} %get-tuple-element.5) | copy-start | bytes 393220

commit v3 on v2

--- a/solution.py
+++ b/solution.py
@@ -52,13 +52,19 @@
     )
 
 
+def gain_of(ref):
+    return ref[...].astype(jnp.float32).reshape(1, -1)
+
+
 def rows_of(index, count):
     return pl.ds(pl.multiple_of(index * count, count), count)
 
 
 def reader_kernel(
-    hidden,
-    gains,
+    hidden_in,
+    ffn_gain_in,
+    final_gain_in,
+    dec_gain_in,
     gate_w,
     up_w,
     down_w,
@@ -66,11 +72,19 @@
     value_w,
     query_w,
     out_w,
+    table_in,
+    ids_in,
+    lengths,
+    memory_out,
+    decoded,
+    hidden,
+    ffn_gain,
+    final_gain,
+    dec_gain,
     table,
     ids,
-    lengths,
     memory,
-    decoded,
+    spread_picks,
     a_own,
     b_own,
     fa,
@@ -98,11 +112,14 @@
     f4,
     f5,
     flat,
+    load_sem,
     a1,
     a2,
     b1,
     b2,
     sends,
+    y_send,
+    y_recv,
     down_send,
     down_recv,
     e_send,
@@ -120,37 +137,56 @@
     f32, bf16 = jnp.float32, jnp.bfloat16
     x, z, n = lax.axis_index(X), lax.axis_index(Z), lax.axis_index(CORE)
     core = {CORE: 1 - n}
+    group = lax.axis_index("groups")
+    parity = lax.rem(group, 2)
+    partner = {"groups": group + 1 - 2 * parity}
     mate = x + 1 - 2 * lax.rem(x, 2)
-    peers = others(X, NX) + others(Z, NZ) + [core]
-    barrier = pltpu.get_barrier_semaphore()
-    for peer in peers:
-        pl.semaphore_signal(barrier, inc=1, device_id=peer, device_id_type=MESH)
-
     ff, proj = gate_w.shape[1], key_w.shape[1]
     width = hidden.shape[1]
     half = width // 2
     rows = hidden.shape[0]
     answers = own_rows.shape[0]
-    at = 0
+    loads, at = [], 0
     for ref in (down_w, key_w, value_w, query_w, out_w):
-        a_own[:, at : at + ref.shape[1]] = ref[...]
+        loads.append((ref, a_own.at[:, at : at + ref.shape[1]]))
         at += ref.shape[1]
-    for c in range(ff // 128):
-        b_own[:, 256 * c : 256 * c + 128] = gate_w[:, 128 * c : 128 * (c + 1)]
-        b_own[:, 256 * c + 128 : 256 * (c + 1)] = up_w[:, 128 * c : 128 * (c + 1)]
+    loads += [(gate_w, b_own.at[:, :ff]), (up_w, b_own.at[:, ff:])]
+    loads += [(ids_in, ids), (table_in.at[:, rows_of(n, half)], table)]
+    shard_loads = len(loads)
+    loads += [(hidden_in, hidden), (ffn_gain_in, ffn_gain)]
+    loads += [(final_gain_in, final_gain), (dec_gain_in, dec_gain)]
+    loads = [
+        pltpu.make_async_copy(src, dst, load_sem.at[k]) for k, (src, dst) in enumerate(loads)
+    ]
+    for load in loads:
+        load.start()
+    peers = others(X, NX) + others(Z, NZ) + [core, partner]
+    barrier = pltpu.get_barrier_semaphore()
+    for peer in peers:
+        pl.semaphore_signal(barrier, inc=1, device_id=peer, device_id_type=MESH)
+    for load in loads[:shard_loads]:
+        load.wait()
 
     vocab_rows = table.shape[0]
-    local_ids = ids[...] - (x * NZ + z) * vocab_rows
-    spot = lax.broadcasted_iota(jnp.int32, (vocab_rows, ids.shape[1]), 0)
-    onehot = (spot == local_ids).astype(f32).astype(bf16)
-    shares = lax.dot_general(
-        onehot,
-        table[:, rows_of(n, half)],
-        (((0,), (0,)), ((), ())),
-        preferred_element_type=f32,
-    ).astype(bf16)
+    spot = lax.broadcasted_iota(jnp.int32, (vocab_rows, answers), 0)
+    for q in range(QUEST):
+        local_ids = ids[q : q + 1] - (x * NZ + z) * vocab_rows
+        shares = lax.dot_general(
+            (spot == local_ids).astype(f32).astype(bf16),
+            table[...],
+            (((0,), (0,)), ((), ())),
+            preferred_element_type=f32,
+        )
+        for i in range(2):
+            for r in range(half // 128):
+                spread_picks[r, pl.ds(2 * q + i, NZ, stride=NX), :] = shares[
+                    NZ * i : NZ * (i + 1), 128 * r : 128 * (r + 1)
+                ]
     for k in range(NZ):
-        picks[k] = shares[NX * k : NX * (k + 1)]
+        for r in range(half // 128):
+            picks[k, :, 128 * r : 128 * (r + 1)] = spread_picks[
+                r, NX * k : NX * (k + 1)
+            ].astype(bf16)
     pl.semaphore_wait(barrier, len(peers))
 
     def block_a(first, second):
@@ -163,33 +199,51 @@
     for index, (src, full, block, axis1, n1, axis2, n2, sem1, sem2) in enumerate(
         ((a_own, fa, block_a, Z, NZ, X, NX, a1, a2), (b_own, fb, block_b, X, NX, Z, NZ, b1, b2))
     ):
-        columns = src.shape[1]
+        total = src.shape[1]
+        share = total // 128 * 2 // 11 * 128 + (128 if index == 0 else 0)
+        columns = total - share
         middle = columns // 256 * 128
-        cuts = (pl.ds(0, middle), pl.ds(middle, columns - middle))
+        start = parity * share
+        cuts = (
+            pl.ds(pl.multiple_of(start, 128), middle),
+            pl.ds(pl.multiple_of(start + middle, 128), columns - middle),
+        )
+        area = pl.ds(pl.multiple_of(start, 128), columns)
+        given = pl.ds(pl.multiple_of(parity * columns, 128), share)
         me1, me2 = lax.axis_index(axis1), lax.axis_index(axis2)
         peers1 = tuple({axis1: turn(me1, d, n1)} for d in (1, -1))
         peers2 = tuple({axis2: turn(me2, d, n2)} for d in (1, -1))
-        plans.append((index, src, full, block, n1, n2, sem1, sem2, cuts, peers1, peers2))
+        plans.append(
+            (index, src, full, block, n1, n2, sem1, sem2, cuts, peers1, peers2, area, given)
+        )
 
     def off(k):
         odd = lax.rem(k, 2)
         return (1 - odd) * (k // 2) - odd * ((k + 1) // 2)
 
+    def hand_over(plan, src, which):
+        index, full, given = plan[0], plan[2], plan[12]
+        remote(
+            src.at[:, given], full.at[which, :, given], y_send.at[index], y_recv.at[index], partner
+        ).start()
+
     def first_stage(plan, t):
-        index, src, full, block, n1, n2, sem1, sem2, cuts, peers1, peers2 = plan
+        index, src, full, block, n1, n2, sem1, sem2, cuts, peers1, peers2, area, given = plan
         send = sends.at[3 * index]
 
         @pl.when(t == 0)
         def _():
-            mine = full.at[block(0, 0)]
+            mine = full.at[block(0, 0), :, area]
+            hand_over(plan, src, block(0, 0))
+            sent = src.at[:, area]
             for d in range(2):
-                remote(src, mine, send, sem1.at[1 + d], peers1[d]).start()
+                remote(sent, mine, send, sem1.at[1 + d], peers1[d]).start()
             for d in range(2):
-                remote(src, mine, send, sem2.at[d, 0, 0], peers2[d]).start()
+                remote(sent, mine, send, sem2.at[d, 0, 0], peers2[d]).start()
 
         @pl.when((t > 0) & (t < n1))
         def _():
-            at = full.at[block(off(t), 0)]
+            at = full.at[block(off(t), 0), :, area]
             remote(at, at, send, sem1.at[t], peers1[0]).wait_recv()
             odd = lax.rem(t, 2)
 
@@ -203,30 +257,34 @@
 
             for d in range(2):
                 remote(at, at, send, sem2.at[d, 0, t], peers2[d]).start()
+            hand_over(plan, full.at[block(off(t), 0)], block(off(t), 0))
 
     def later_stage(plan, t, h):
-        index, src, full, block, n1, n2, sem1, sem2, cuts, peers1, peers2 = plan
+        index, src, full, block, n1, n2, sem1, sem2, cuts, peers1, peers2, area, given = plan
         last = n2 // 2
         k = t - 2 * h
 
         @pl.when((k >= 0) & (k < n1))
         def _():
             for d in range(2):
-                at = full.at[block(off(k), -h if d == 0 else h)]
+                which = block(off(k), -h if d == 0 else h)
+                at = full.at[which, :, area]
+                part = full.at[which, :, cuts[d]]
                 if h == last:
-                    part = at.at[:, cuts[d]]
                     remote(
                         part, part, sends.at[3 * index + 1 + d], sem2.at[d, h - 1, k], peers2[d]
                     ).wait_recv()
+                    if d == 1:
+                        hand_over(plan, full.at[which], which)
                     continue
                 remote(at, at, sends.at[3 * index], sem2.at[d, h - 1, k], peers2[d]).wait_recv()
                 if h + 1 == last:
-                    part = at.at[:, cuts[d]]
                     remote(
                         part, part, sends.at[3 * index + 1 + d], sem2.at[d, h, k], peers2[d]
                     ).start()
                 else:
                     remote(at, at, sends.at[3 * index], sem2.at[d, h, k], peers2[d]).start()
+                hand_over(plan, full.at[which], which)
 
     def tick(t, carry):
         for plan in plans:
@@ -245,11 +303,13 @@
         first_copies.append(copy)
     lax.fori_loop(0, 2, tick, 0)
 
+    for load in loads[shard_loads:]:
+        load.wait()
     resid_in = hidden[...].astype(f32)
     mean_square = jnp.mean(resid_in * resid_in, axis=-1, keepdims=True)
-    enc[...] = (resid_in * lax.rsqrt(mean_square + EPS) * gains[0:1]).astype(bf16)
-    fa[x * NZ + z] = a_own[...]
-    fb[x * NZ + z] = b_own[...]
+    enc[...] = (resid_in * lax.rsqrt(mean_square + EPS) * gain_of(ffn_gain)).astype(bf16)
+    for index, src, full, block, *_, area, given in plans:
+        full[block(0, 0), :, area] = src[:, area]
     lax.fori_loop(2, 5, tick, 0)
 
     total = picks[z].astype(f32)
@@ -307,19 +367,23 @@
                 )
     embedded = own_rows[...]
     mean_square = jnp.mean(embedded * embedded, axis=-1, keepdims=True)
-    dec_in = (embedded * lax.rsqrt(mean_square + EPS) * gains[2:3]).astype(bf16)
+    dec_in = (embedded * lax.rsqrt(mean_square + EPS) * gain_of(dec_gain)).astype(bf16)
     lax.fori_loop(16, NX + NZ, tick, 0)
 
-    for index, src, full, block, n1, n2, sem1, sem2, cuts, peers1, peers2 in plans:
+    for index, src, full, block, n1, n2, sem1, sem2, cuts, peers1, peers2, area, given in plans:
         count = (n1 - 1) + 2 * n1 * (n2 // 2 - 1)
-        whole = full.at[pl.ds(0, count)]
+        whole = full.at[:, :, given]
+        remote(whole, whole, y_send.at[index], y_recv.at[index], partner).wait()
+        whole = full.at[pl.ds(0, count), :, area]
         remote(whole, whole, sends.at[3 * index], sem1.at[0], peers1[0]).wait_send()
         for d in range(2):
             piece = full.at[pl.ds(0, n1), :, cuts[d]]
             remote(piece, piece, sends.at[3 * index + 1 + d], sem1.at[0], peers1[0]).wait_send()
 
     def ffn(c, carry):
-        weight = fb[:, :, rows_of(c, 256)].reshape(width, 256)
+        gate_at = pl.ds(pl.multiple_of(c * 128, 128), 128)
+        up_at = pl.ds(pl.multiple_of(ff + c * 128, 128), 128)
+        weight = jnp.concatenate((fb[:, :, gate_at], fb[:, :, up_at]), axis=2).reshape(width, 256)
         both = dot(enc[...], weight)
         value = jax.nn.gelu(both[:, :128], approximate=True) * both[:, 128:]
         inner[:, rows_of(c, 128)] = value.astype(bf16)
@@ -341,11 +405,14 @@
         down_other[c] = resid
         squares = squares + jnp.sum(resid * resid, axis=-1, keepdims=True)
     scale = lax.rsqrt(squares * (1.0 / width) + EPS)
+    gain = gain_of(final_gain)
     for c in range(width // 256):
         cols = slice(256 * c, 256 * (c + 1))
-        memory[:, cols] = (down_other[c] * scale * gains[1:2, cols]).astype(bf16)
+        memory[:, cols] = (down_other[c] * scale * gain[:, cols]).astype(bf16)
     for copy in copies:
         copy.wait_send()
+    store = pltpu.make_async_copy(memory, memory_out, load_sem.at[0])
+    store.start()
 
     mem = memory[...]
     keys = dot(mem, fa[:, :, ff : ff + proj].reshape(width, proj)).astype(bf16)
@@ -452,19 +519,27 @@
                 ].astype(bf16)
     for copy in copies:
         copy.wait_send()
-
-
-def reader(hidden, gains, shards, table, ids, lengths, answers):
+    store.wait()
+
+
+def reader(hidden, gains, shards, table, ids, lengths):
     gate_w, up_w, down_w, key_w, value_w, query_w, out_w = shards
     dma = pltpu.SemaphoreType.DMA
     f32, bf16 = jnp.float32, jnp.bfloat16
     blocks = NX * NZ
+    answers = ids.shape[1]
     rows, width = hidden.shape
     ff, proj, half = gate_w.shape[1], key_w.shape[1], width // 2
     a_width, b_width = ff + 4 * proj, 2 * ff
     chunks = width // 256
     vmem = pltpu.VMEM
     scratch = [
+        vmem((rows, width), bf16),
+        *[vmem(gain.shape, bf16) for gain in gains],
+        vmem((table.shape[0], half), bf16),
+        vmem(ids.shape, ids.dtype),
+        vmem((rows, width), bf16),
+        vmem((half // 128, NX * NZ, 128), f32),
         vmem((8, a_width), bf16),
         vmem((8, b_width), bf16),
         vmem((blocks, 8, a_width), bf16),
@@ -492,11 +567,14 @@
         vmem((QUEST, 8, 128), bf16),
         vmem((NZ, QUEST, 8, 128), bf16),
         vmem((NZ * QUEST * 8, 128), f32),
+        dma((len(shards) + 6,)),
         dma((NZ,)),
         dma((2, NX // 2, NZ)),
         dma((NX,)),
         dma((2, NZ // 2, NX)),
         dma((6,)),
+        dma((2,)),
+        dma((2,)),
         dma((chunks,)),
         dma((chunks,)),
         dma((NZ,)),
@@ -517,14 +595,15 @@
             jax.ShapeDtypeStruct((rows, width), bf16),
             jax.ShapeDtypeStruct((QUEST * answers, half), bf16),
         ),
-        in_specs=[pl.BlockSpec(memory_space=vmem)] * 11 + [pl.BlockSpec(memory_space=pltpu.SMEM)],
-        out_specs=(pl.BlockSpec(memory_space=vmem),) * 2,
+        in_specs=[pl.BlockSpec(memory_space=pl.ANY)] * 13
+        + [pl.BlockSpec(memory_space=pltpu.SMEM)],
+        out_specs=(pl.BlockSpec(memory_space=pl.ANY), pl.BlockSpec(memory_space=vmem)),
         scratch_shapes=scratch,
         compiler_params=pltpu.CompilerParams(
             collective_id=1, has_side_effects=True, vmem_limit_bytes=60 * 2**20
         ),
         name="reader",
-    )(hidden, gains, *shards, table, ids, lengths)
+    )(hidden, *gains, *shards, table, ids, lengths)
 
 
 def per_device(
@@ -543,10 +622,9 @@
     lengths,
     answer_ids,
 ):
-    gains = jnp.stack((ffn_gain, final_gain, dec_gain)).astype(jnp.float32)
-    ids = answer_ids.reshape(NX, NZ).T.reshape(1, NX * NZ)
+    gains = (ffn_gain, final_gain, dec_gain)
     shards = (wi_gate, wi_up, wo_down.T, key_w, value_w, query_w, out_w.T)
-    return reader(hidden_in, gains, shards, embed, ids, lengths, answer_ids.shape[1])
+    return reader(hidden_in, gains, shards, embed, answer_ids, lengths)
 
 
 def solution(mesh):

time: 183 us -> 172 us (0.940)
  Pallas kernels: 176 us -> 168 us
  local copies, waits for them, and re-layouts: 5.63 us -> 2.78 us
    pallas_call x1, Pallas kernels: 176 us -> 168 us  [reader(): pl.pallas_call(reader_kernel, out_shape=(jax.ShapeDtypeStruct((rows, widt...]
    unnamed x12 -> x4, local copies, waits for them, and re-layouts: 4.87 us -> 2.78 us
where the time goes in v3:
time: 172 us; the launch traced here: 171 us
  Pallas kernels  168 us (98%)
  local copies, waits for them, and re-layouts  2.78 us (2%)
    pallas_call x1, Pallas kernels, reader(): pl.pallas_call(reader_kernel, out_shape=(jax.ShapeDtypeStruct((rows, widt...  168 us

profile of v3, /device:TPU:65, one launch (start us, length us, event | category | flops | bytes accessed | tf_op | source)
XLA Modules:
  0.0 171.4 jit_solution(1342225771199470341)
XLA Ops:
  0.6 168.0 %reader.1 = (bf16[400,1024]{1,0:T(8,128)(2,1)}, bf16[128,512]{1,0:T(8,128)(2,1)}) custom-call(bf16[400,1024]{1,0:T(8,128)(2,1)} %hidden_in.1, bf16[1024]{0:T(1024)(128)(2,1)} %ffn_gain_in.1, bf16[1024]{0:T(1024)(128)(2,1)} %final_gain_in.1, bf16[1024]{0:T(1024)(128)(2,1)} %dec_gain_in.1, bf16[8,1408]{1,0:T(8,128)(2,1)} %gate_w.1, bf16[8,1408]{1,0:T(8,128)(2,1)} %up_w.1, ...), custom_call_target="tpu_custom_call" | custom-call | tf_op jit(solution)/shard_map/reader/pallas_call | solution.py:592
  168.6 0.0 copy-start
  168.6 2.1 %copy.18 = bf16[400,1024]{1,0:T(8,128)(2,1)} copy(bf16[400,1024]{1,0:T(8,128)(2,1)} %get-tuple-element.4) | data formatting | bytes 1638400
  170.7 0.0 copy-done
  170.7 0.7 copy.19
Async XLA Ops:
  168.6 2.1 %copy-start = (bf16[128,512]{1,0:T(8,128)(2,1)S(1)}, bf16[128,512]{1,0:T(8,128)(2,1)}, u32[]{:S(2)}) copy-start(bf16[128,512]{1,0:T(8,128)(2,1)} %get-tuple-element.5) | copy-start | bytes 393220

commit v4 on v3

--- a/solution.py
+++ b/solution.py
@@ -99,6 +99,7 @@
     e2,
     e3_src,
     e3,
+    e4,
     emb,
     own_rows,
     part,
@@ -200,7 +201,7 @@
         ((a_own, fa, block_a, Z, NZ, X, NX, a1, a2), (b_own, fb, block_b, X, NX, Z, NZ, b1, b2))
     ):
         total = src.shape[1]
-        share = total // 128 * 2 // 11 * 128 + (128 if index == 0 else 0)
+        share = total // 128 * 2 // 9 * 128
         columns = total - share
         middle = columns // 256 * 128
         start = parity * share
@@ -335,30 +336,29 @@
         total = total + e2[d]
     for copy in copies:
         copy.wait_send()
-    e3_src[...] = total
-    e3[rows_of(z, 8)] = total
+    e3_src[...] = total.astype(bf16)
+    e3[z] = total.astype(bf16)
     copies = []
     for d in range(1, NZ):
-        copy = remote(
-            e3_src, e3.at[rows_of(z, 8)], e_send.at[d], e_r3.at[d], {Z: turn(z, d, NZ)}
-        )
+        copy = remote(e3_src, e3.at[z], e_send.at[d], e_r3.at[d], {Z: turn(z, d, NZ)})
         copy.start()
         copies.append(copy)
     lax.fori_loop(8, 12, tick, 0)
 
     for d in range(1, NZ):
-        slot = e3.at[rows_of(turn(z, -d, NZ), 8)]
+        slot = e3.at[turn(z, -d, NZ)]
         remote(slot, slot, e_send.at[d], e_r3.at[d], {Z: turn(z, d, NZ)}).wait_recv()
     for copy in copies:
         copy.wait_send()
-    copy = remote(e3, emb.at[rows_of(n, 8 * NZ)], e_send.at[0], e_r4.at[0], core)
+    copy = remote(e3, e4.at[n], e_send.at[0], e_r4.at[0], core)
     copy.start()
-    emb[rows_of(n, 8 * NZ)] = e3[...]
+    e4[n] = e3[...]
     lax.fori_loop(12, 16, tick, 0)
 
-    slot = emb.at[rows_of(1 - n, 8 * NZ)]
+    slot = e4.at[1 - n]
     remote(slot, slot, e_send.at[0], e_r4.at[0], core).wait_recv()
     copy.wait_send()
+    emb[...] = e4[...].astype(f32).reshape(emb.shape)
     for h in range(2):
         for r in range(half // 128):
             for i in range(2):
@@ -552,8 +552,9 @@
         vmem((NZ, NX, half), bf16),
         vmem((QUEST, 8, 128), f32),
         vmem((NX, 8, 128), f32),
-        vmem((8, 128), f32),
-        vmem((8 * NZ, 128), f32),
+        vmem((8, 128), bf16),
+        vmem((NZ, 8, 128), bf16),
+        vmem((2, NZ, 8, 128), bf16),
         vmem((16 * NZ, 128), f32),
         vmem((answers, width), f32),
         vmem((16 * NZ, 128), f32),

time: 172 us -> 169 us (0.983)
  Pallas kernels: 168 us -> 165 us
    pallas_call x1, Pallas kernels: 168 us -> 165 us  [reader(): pl.pallas_call(reader_kernel, out_shape=(jax.ShapeDtypeStruct((rows, widt...]
where the time goes in v4:
time: 169 us
  Pallas kernels  165 us (98%)
  local copies, waits for them, and re-layouts  2.78 us (2%)
    pallas_call x1, Pallas kernels, reader(): pl.pallas_call(reader_kernel, out_shape=(jax.ShapeDtypeStruct((rows, widt...  165 us

profile of v4, /device:TPU:65, one launch (start us, length us, event | category | flops | bytes accessed | tf_op | source)
XLA Modules:
  0.0 168.6 jit_solution(469272225102213760)
XLA Ops:
  0.6 165.1 %reader.1 = (bf16[400,1024]{1,0:T(8,128)(2,1)}, bf16[128,512]{1,0:T(8,128)(2,1)}) custom-call(bf16[400,1024]{1,0:T(8,128)(2,1)} %hidden_in.1, bf16[1024]{0:T(1024)(128)(2,1)} %ffn_gain_in.1, bf16[1024]{0:T(1024)(128)(2,1)} %final_gain_in.1, bf16[1024]{0:T(1024)(128)(2,1)} %dec_gain_in.1, bf16[8,1408]{1,0:T(8,128)(2,1)} %gate_w.1, bf16[8,1408]{1,0:T(8,128)(2,1)} %up_w.1, ...), custom_call_target="tpu_custom_call" | custom-call | tf_op jit(solution)/shard_map/reader/pallas_call | solution.py:593
  165.8 0.0 copy-start
  165.8 2.1 %copy.18 = bf16[400,1024]{1,0:T(8,128)(2,1)} copy(bf16[400,1024]{1,0:T(8,128)(2,1)} %get-tuple-element.4) | data formatting | bytes 1638400
  167.9 0.0 copy-done
  167.9 0.7 copy.19
Async XLA Ops:
  165.8 2.1 %copy-start = (bf16[128,512]{1,0:T(8,128)(2,1)S(1)}, bf16[128,512]{1,0:T(8,128)(2,1)}, u32[]{:S(2)}) copy-start(bf16[128,512]{1,0:T(8,128)(2,1)} %get-tuple-element.5) | copy-start | bytes 393220
